TPU v7x, 16 devices: a whole 2x2x2 slice. The times are simulated.
16 devices in a mesh: outer: 4 (over z, y), inner: 4 (over x, core).
Axes of the slice: x: 2, y: 2, z: 2, core: 2. Of those that a mesh axis runs over, the one named last changes fastest.
Arguments:
- g_emb: float32 [16, 4096, 768], P(('outer', 'inner'))
- g_qkv: float32 [16, 2, 768, 2304], P(('outer', 'inner'))
- g_o: float32 [16, 2, 768, 768], P(('outer', 'inner'))
- g_w1: float32 [16, 2, 768, 3072], P(('outer', 'inner'))
- g_w2: float32 [16, 2, 3072, 768], P(('outer', 'inner'))
- g_bqkv: float32 [16, 2, 2304], P(('outer', 'inner'))
- g_b1: float32 [16, 2, 3072], P(('outer', 'inner'))
- g_dvec: float32 [16, 2, 6, 768], P(('outer', 'inner'))
- m: float32 [17321472], P(('outer', 'inner'))
- v: float32 [17321472], P(('outer', 'inner'))
- w: float32 [17321472], P(('outer', 'inner'))
- lr: float32 [], replicated
- beta1: float32 [], replicated
- beta2: float32 [], replicated
- eps: float32 [], replicated
- step: int32 [], replicated
Outputs:
- output 1: float32 [17321472], P(('outer', 'inner'))
- output 2: float32 [17321472], P(('outer', 'inner'))
- output 3: float32 [17321472], P(('outer', 'inner'))
- output 4: bfloat16 [4096, 768], replicated
- output 5: bfloat16 [2, 768, 2304], replicated
- output 6: bfloat16 [2, 768, 768], replicated
- output 7: bfloat16 [2, 768, 3072], replicated
- output 8: bfloat16 [2, 3072, 768], replicated
- output 9: bfloat16 [2, 2304], replicated
- output 10: bfloat16 [2, 3072], replicated
- output 11: bfloat16 [2, 6, 768], replicated
All inputs are finite; a program needn't handle non-finite values.
Results may differ from a plain program's by a relative error of at most 0.001.
Values are sent between devices in bfloat16 or wider.
A program may use at most 1 GiB of HBM per device.

v0:
```python
import math
import jax
import jax.numpy as jnp
from jax import lax
from jax.sharding import PartitionSpec as P

AXES = ("outer", "inner")


def adam_update(g, m, v, w, lr, beta1, beta2, eps, step):
    t = step.astype(jnp.float32)
    m_new = beta1 * m + (1.0 - beta1) * g
    v_new = beta2 * v + (1.0 - beta2) * (g * g)
    m_hat = m_new / (1.0 - beta1 ** t)
    v_hat = v_new / (1.0 - beta2 ** t)
    w_new = w - lr * m_hat / (jnp.sqrt(v_hat) + eps)
    return m_new, v_new, w_new


def restore(flat, shapes):
    outs = []
    start = 0
    for shape in shapes:
        n = math.prod(shape)
        outs.append(flat[start:start + n].reshape(shape))
        start = start + n
    return tuple(outs)


def solution(mesh):
    p = mesh.shape["outer"] * mesh.shape["inner"]

    def body(g_emb, g_qkv, g_o, g_w1, g_w2, g_bqkv, g_b1, g_dvec, m, v, w, lr, beta1, beta2, eps, step):
        grads = (g_emb, g_qkv, g_o, g_w1, g_w2, g_bqkv, g_b1, g_dvec)
        shapes = tuple(x.shape[1:] for x in grads)
        local = jnp.concatenate([x.reshape(-1) for x in grads])
        g = lax.psum_scatter(local, AXES, scatter_dimension=0, tiled=True) / p
        m_new, v_new, w_new = adam_update(g, m, v, w, lr, beta1, beta2, eps, step)
        wb = lax.all_gather(w_new.astype(jnp.bfloat16), AXES, axis=0, tiled=True)
        return (m_new, v_new, w_new) + restore(wb, shapes)

    g3 = P(AXES, None, None)
    g4 = P(AXES, None, None, None)
    flat = P(AXES)
    rep = P()
    in_specs = (g3, g4, g4, g4, g4, g3, g3, g4, flat, flat, flat, rep, rep, rep, rep, rep)
    out_specs = (flat, flat, flat, rep, rep, rep, rep, rep, rep, rep, rep)
    return jax.shard_map(body, mesh=mesh, in_specs=in_specs, out_specs=out_specs, check_vma=False)
```

profile of v0, /device:TPU:0, one launch (start us, length us, event | category | flops | bytes accessed | tf_op | source)
XLA Modules:
  0.0 1219.0 jit_solution(16180200717736468978)
XLA Ops:
  7.2 0.0 all-reduce.7.cloned.1.call-start
  7.2 13.3 %reshape.82 = f32[3145728]{0:T(1024)} reshape(f32[1,4096,768]{2,1,0:T(8,128)} %param.16) | data formatting | bytes 25165824 | tf_op jit(solution)/shard_map/reshape | solution.py:36
  20.5 10.0 constant_dynamic-update-slice_fusion.7
  30.6 15.2 %reshape.83 = f32[3538944]{0:T(1024)} reshape(f32[1,2,768,2304]{3,2,1,0:T(8,128)} %param.17) | data formatting | bytes 28311552 | tf_op jit(solution)/shard_map/reshape | solution.py:36
  45.7 5.7 reshape.84
  51.4 17.8 %copy.31 = f32[192,24,8,128]{3,1,2,0:T(8,128)} copy(f32[192,24,8,128]{3,2,1,0:T(8,128)} %bitcast.15) | data formatting | bytes 37748736
  69.2 19.7 %reshape.86 = f32[4718592]{0:T(1024)} reshape(f32[1,2,3072,768]{3,2,1,0:T(8,128)} %param.20) | data formatting | bytes 37748736 | tf_op jit(solution)/shard_map/reshape | solution.py:36
  89.0 0.0 copy-start
  89.0 0.0 slice-start.5
  89.0 0.0 slice-start.6
  89.1 0.0 slice-start.7
  89.1 0.0 slice-start.8
  89.1 11.8 constant_dynamic-update-slice_fusion.6
  100.9 2.6 constant_dynamic-update-slice_fusion.5
  103.4 1.3 slice-done.6
  104.7 1.2 slice-done.7
  105.9 1.2 slice-done.8
  107.1 0.8 slice-done.9
  107.9 9.4 constant_dynamic-update-slice_fusion.4
  117.3 0.0 slice-done
  117.4 0.0 slice-done.2
  117.4 1.8 slice-done.3
  119.2 0.6 slice-done.4
  119.8 6.6 constant_dynamic-update-slice_fusion.3
  126.4 1.4 constant_dynamic-update-slice_fusion.2
  127.8 1.4 constant_dynamic-update-slice_fusion.1
  129.1 1.4 constant_dynamic-update-slice_fusion
  130.5 0.0 all-reduce.7.cloned.1.call-update
  130.6 0.0 all-reduce.5.cloned.1.call-start
  134.0 606.6 %all-reduce.7.cloned.1.call-done = f32[17321472]{0:T(1024)} async-done(((f32[17321472]{0:T(1024)}), f32[17321472]{0:T(1024)}) %all-reduce.7.cloned.1.call-update) | async-done | bytes 69285904
  740.5 10.6 fusion
  751.1 11.2 broadcast.2
  762.4 33.4 %dynamic-update-slice = bf16[17321472]{0:T(1024)(128)(2,1)} dynamic-update-slice(bf16[17321472]{0:T(1024)(128)(2,1)} %broadcast.2, bf16[1082592]{0:T(1024)(128)(2,1)S(1)} %get-tuple-element.33, u32[]{:T(128)S(6)} %multiply.4) | dynamic-update-slice | bytes 4330372
  795.8 0.0 all-reduce.5.cloned.1.call-update
  795.8 325.4 %all-reduce.5.cloned.1.call-done = bf16[17321472]{0:T(1024)(128)(2,1)} async-done(((bf16[17321472]{0:T(1024)(128)(2,1)}), bf16[17321472]{0:T(1024)(128)(2,1)}) %all-reduce.5.cloned.1.call-update) | async-done | bytes 34642960
  1121.2 14.6 %fusion.1 = (bf16[4718592]{0:T(1024)(128)(2,1)}, bf16[4718592]{0:T(1024)(128)(2,1)}) fusion(bf16[17321472]{0:T(1024)(128)(2,1)} %all-reduce.5.cloned.1.call-done), kind=kLoop, calls=%fused_computation.12 | loop fusion | bytes 37748736 | tf_op jit(solution)/shard_map/slice | solution.py:25
  1135.8 14.8 %reshape.92 = bf16[2,768,3072]{2,1,0:T(8,128)(2,1)} reshape(bf16[4718592]{0:T(1024)(128)(2,1)} %get-tuple-element.38) | data formatting | bytes 18874368 | tf_op jit(solution)/shard_map/reshape | solution.py:25
  1150.6 16.8 %reshape.93 = bf16[2,3072,768]{2,1,0:T(8,128)(2,1)} reshape(bf16[4718592]{0:T(1024)(128)(2,1)} %get-tuple-element.37) | data formatting | bytes 18874368 | tf_op jit(solution)/shard_map/reshape | solution.py:25
  1167.3 6.3 slice.55
  1173.7 13.8 %reshape.90 = bf16[2,768,2304]{2,1,0:T(8,128)(2,1)} reshape(bf16[3538944]{0:T(1024)(128)(2,1)} %slice.55) | data formatting | bytes 14155776 | tf_op jit(solution)/shard_map/reshape | solution.py:25
  1187.5 6.4 slice.54
  1193.9 11.7 slice.45
  1205.6 3.2 reshape.91
  1208.8 0.7 slice.61
  1209.6 0.6 copy.30
  1210.2 0.7 slice.60
  1210.9 0.6 reshape.95
  1211.5 0.6 reshape.94
  (26 shorter events, 0.1 us)
Async XLA Ops:
  7.2 733.4 %all-reduce.7.cloned.1.call-start = ((), (), s32[]{:S(2)}) async-start(), calls=%async_computation.1 | async-start | bytes 138575872
  69.2 19.7 %copy-start.3 = (f32[1,2,2304]{2,1,0:T(2,128)S(1)}, f32[1,2,2304]{2,1,0:T(2,128)}, u32[]{:S(2)}) copy-start(f32[1,2,2304]{2,1,0:T(2,128)} %param.21) | copy-start | bytes 55300
  69.2 19.7 %copy-start.2 = (f32[1,2,3072]{2,1,0:T(2,128)S(1)}, f32[1,2,3072]{2,1,0:T(2,128)}, u32[]{:S(2)}) copy-start(f32[1,2,3072]{2,1,0:T(2,128)} %param.22) | copy-start | bytes 73732
  69.2 19.8 %copy-start.1 = (f32[1,2,6,768]{3,1,2,0:T(2,128)S(1)}, f32[1,2,6,768]{3,1,2,0:T(2,128)}, u32[]{:S(2)}) copy-start(f32[1,2,6,768]{3,1,2,0:T(2,128)} %param.23) | copy-start | bytes 110596
  89.0 11.8 copy-start
  89.0 14.4 %slice-start.5 = ((s8[18874368]{0:T(1024)(128)(4,1)}), s8[4194304]{0:T(1024)(128)(4,1)S(1)}, s32[]{:S(2)}) async-start(s8[18874368]{0:T(1024)(128)(4,1)} %bitcast.12), calls=%async_computation.7 | async-start | bytes 8388608
  89.0 15.7 %slice-start.6 = ((s8[18874368]{0:T(1024)(128)(4,1)}), s8[4194304]{0:T(1024)(128)(4,1)S(1)}, s32[]{:S(2)}) async-start(s8[18874368]{0:T(1024)(128)(4,1)} %bitcast.12), calls=%async_computation.8 | async-start | bytes 8388608
  89.1 16.9 %slice-start.7 = ((s8[18874368]{0:T(1024)(128)(4,1)}), s8[4194304]{0:T(1024)(128)(4,1)S(1)}, s32[]{:S(2)}) async-start(s8[18874368]{0:T(1024)(128)(4,1)} %bitcast.12), calls=%async_computation.9 | async-start | bytes 8388608
  89.1 18.1 %slice-start.8 = ((s8[18874368]{0:T(1024)(128)(4,1)}), s8[4194304]{0:T(1024)(128)(4,1)S(1)}, s32[]{:S(2)}) async-start(s8[18874368]{0:T(1024)(128)(4,1)} %bitcast.12), calls=%async_computation.10 | async-start | bytes 8388608
  100.9 7.1 slice-start.9
  103.4 13.9 %slice-start = ((s8[18874368]{0:T(1024)(128)(4,1)}), s8[4194304]{0:T(1024)(128)(4,1)S(1)}, s32[]{:S(2)}) async-start(s8[18874368]{0:T(1024)(128)(4,1)} %bitcast.10), calls=%async_computation.2 | async-start | bytes 8388608
  107.9 9.4 slice-start.1
  107.9 9.4 slice-start.2
  107.9 11.3 slice-start.3
  107.9 11.9 slice-start.4
  130.6 990.7 %all-reduce.5.cloned.1.call-start = ((), (), s32[]{:S(2)}) async-start(), calls=%async_computation | async-start | bytes 69287936
  1193.9 11.7 slice-start.10
  1193.9 17.6 %slice-start.11 = ((bf16[17321472]{0:T(1024)(128)(2,1)}), bf16[4608]{0:T(1024)(128)(2,1)S(1)}, s32[]{:S(2)}) async-start(bf16[17321472]{0:T(1024)(128)(2,1)} %all-reduce.5.cloned.1.call-done), calls=%async_computation.13 | async-start | bytes 20480 | tf_op jit(solution)/shard_map/slice | solution.py:25
Sparse Core Ops, SparseCore 0:
  130.7 609.8 all-reduce.6
  795.9 325.2 all-reduce.4
where the time goes:
time: 1230 us; the launch traced here: 1220 us
  waiting for transfers between devices  932 us (76%)
  local copies, waits for them, and re-layouts  259 us (21%)
  between operations  17.5 us (1%)
    unnamed x4, waiting for transfers between devices  932 us
    unnamed x41, local copies, waits for them, and re-layouts  113 us
    reshape x6, local copies, waits for them, and re-layouts, body(): local = jnp.concatenate([x.reshape(-1) for x in grads])  53.9 us
    reshape x6, local copies, waits for them, and re-layouts, restore(): outs.append(flat[start:start + n].reshape(shape))  49.8 us
    slice x11, local copies, waits for them, and re-layouts, restore(): outs.append(flat[start:start + n].reshape(shape))  40.5 us
  transfers between devices with their start and end apart: 2, of which 2 were waited for; matrix products, arithmetic and copies ran while one was open for 0% of the time, Pallas kernels for 0%

commit v1 on v0

v1 whole, which is shorter than its diff:
```python
import functools
import math

import jax
import jax.numpy as jnp
from jax import lax
from jax.experimental import pallas as pl
from jax.experimental.pallas import tpu as pltpu
from jax.sharding import PartitionSpec as P

AXES = ("outer", "inner")
MESH = pl.DeviceIdType.MESH
ANY = pl.BlockSpec(memory_space=pl.ANY)
LANES = 128
TILE = 16
VMEM_LIMIT = 63 * 1024 * 1024
BF = jnp.bfloat16
F32 = jnp.float32

ORDER = ((1, 1), (1, 0), (0, 1), (0, 0))


class Plan:
    def __init__(self, shapes, p):
        self.p = p
        self.sizes = [math.prod(s) for s in shapes]
        self.total = sum(self.sizes)
        self.shard = self.total // p
        tile = TILE * LANES
        g = math.gcd(self.shard, tile)
        self.num, self.den = self.shard // g, tile // g
        tiles = -(-(self.shard + tile - g) // tile)
        self.unit = -(-tiles // 3) * TILE
        self.window = 3 * self.unit
        self.rows = self.first(p - 1) * TILE + self.window
        self.big = []
        start = 0
        for s, n in zip(shapes, self.sizes):
            if s[-2] % TILE == 0:
                self.big.append((n // s[-1], s[-1] // LANES, start // LANES))
                start += n
        self.small_row = start // LANES
        self.small_size = self.total - start

    def first(self, r):
        if isinstance(r, int):
            return r * self.num // self.den
        return lax.div(r * self.num, self.den)

    def chunks(self, target):
        out = []
        for k, (rows, nj, flat) in enumerate(self.big):
            step = max(c for c in range(TILE, rows + 1, TILE) if rows % c == 0 and c * nj <= target)
            for r in range(0, rows, step):
                out.append((k, r, step, nj, flat + r * nj))
        return out


def group_rows(rows, nj):
    best = TILE
    for c in (16, 32, 64):
        if rows % c == 0 and c * nj <= 384:
            best = c
    return best


def flatten_kernel(plan, work, depth, *refs):
    n = len(plan.big)
    xs, small, f_ref, outs, ins = refs[:n], refs[n], refs[n + 1], refs[n + 2], refs[n + 3:2 * n + 3]
    in_sem, out_sem, small_sem = refs[2 * n + 3:]

    tail = pltpu.make_async_copy(small, f_ref.at[pl.ds(plan.small_row, small.shape[0])], small_sem)
    tail.start()

    def load(i):
        k, r, rows, nj, _ = work[i]
        return pltpu.make_async_copy(xs[k].at[pl.ds(r, rows)], ins[k].at[i % depth], in_sem.at[i % depth])

    def store(i):
        k, r, rows, nj, flat = work[i]
        return pltpu.make_async_copy(
            outs.at[i % depth, pl.ds(0, rows * nj)], f_ref.at[pl.ds(flat, rows * nj)], out_sem.at[i % depth]
        )

    for i in range(min(depth, len(work))):
        load(i).start()
    for i, (k, r, rows, nj, flat) in enumerate(work):
        slot = i % depth
        load(i).wait()
        if i >= depth:
            store(i - depth).wait()
        step = group_rows(rows, nj)

        def body(g, _, k=k, slot=slot, nj=nj, step=step):
            for h in range(0, step, 8):
                src = pl.multiple_of(g * step + h, 8)
                dst = pl.multiple_of(src * nj, 8)
                for j in range(nj):
                    outs[slot, pl.ds(dst + j, 8, stride=nj), :] = ins[k][slot, pl.ds(src, 8), j * LANES:(j + 1) * LANES]
            return 0

        lax.fori_loop(0, rows // step, body, 0)
        store(i).start()
        if i + depth < len(work):
            load(i + depth).start()
    for i in range(max(0, len(work) - depth), len(work)):
        store(i).wait()
    tail.wait()


def flatten(plan, grads):
    n = len(plan.big)
    depth = 4
    work = plan.chunks(3456)
    xs = [x.reshape(rows, nj * LANES) for x, (rows, nj, _) in zip(grads, plan.big)]
    small = jnp.concatenate([x.reshape(-1) for x in grads[n:]])
    pad = (plan.rows - plan.small_row) * LANES - plan.small_size
    small = jnp.pad(small, (0, pad)).reshape(-1, LANES)
    step = {w[0]: w[2] for w in work}
    size = max(w[2] * w[3] for w in work)
    return pl.pallas_call(
        functools.partial(flatten_kernel, plan, work, depth),
        out_shape=jax.ShapeDtypeStruct((plan.rows, LANES), F32),
        in_specs=[ANY] * (n + 1),
        out_specs=ANY,
        scratch_shapes=[pltpu.VMEM((depth, size, LANES), F32)]
        + [pltpu.VMEM((depth, step[k], plan.big[k][1] * LANES), F32) for k in range(n)]
        + [pltpu.SemaphoreType.DMA((depth,)), pltpu.SemaphoreType.DMA((depth,)), pltpu.SemaphoreType.DMA],
        compiler_params=pltpu.CompilerParams(vmem_limit_bytes=VMEM_LIMIT),
        name="flatten",
    )(*xs, small)


class Place:
    def __init__(self):
        o, i = lax.axis_index("outer"), lax.axis_index("inner")
        self.bits = [lax.div(o, 2), lax.rem(o, 2), lax.div(i, 2)]
        self.core = lax.rem(i, 2)

    def flipped(self, d):
        b = list(self.bits)
        b[d] = 1 - b[d]
        return (b[0] * 2 + b[1], b[2] * 2 + self.core)

    def partner(self):
        return (self.bits[0] * 2 + self.bits[1], self.bits[2] * 2 + 1 - self.core)

    def owner(self, dims, e, core):
        b = list(self.bits)
        for d, flip in zip(dims, e):
            if flip:
                b[d] = 1 - b[d]
        return b[0] * 8 + b[1] * 4 + b[2] * 2 + core


def dims_of(k):
    return (k, (k + 1) % 3, (k + 2) % 3)


def meet(place):
    barrier = pltpu.get_barrier_semaphore()
    peers = [place.partner()] + [place.flipped(d) for d in range(3)]
    for peer in peers:
        pl.semaphore_signal(barrier, inc=1, device_id=peer, device_id_type=MESH)
    pl.semaphore_wait(barrier, len(peers))


def remote(src, dst, send, recv, dev):
    return pltpu.make_async_remote_copy(
        src_ref=src, dst_ref=dst, send_sem=send, recv_sem=recv, device_id=dev, device_id_type=MESH
    )


def rs_kernel(plan, f_ref, g_ref, late_ref, early, r1, r2, r3, own, oth, *sems):
    (own_sem, oth_sem, out_sem, d_send, d_recv, s1_send, s1_recv, s2_send, s2_recv, s3_send, s3_recv) = sems
    u = plan.unit
    place = Place()
    partner = place.partner()
    units = [(k, (1,) + e) for e in ORDER for k in range(3)]
    units += [(k, (0,) + e) for e in ORDER for k in range(3)]

    def source(n, core):
        k, e = units[n]
        row = plan.first(place.owner(dims_of(k), e, core)) * TILE + k * u
        return f_ref.at[pl.ds(pl.multiple_of(row, TILE), u)]

    def exchange(n):
        dst = early.at[n] if n < 12 else late_ref.at[n - 12]
        return remote(source(n, 1 - place.core), dst, d_send.at[n], d_recv.at[n], partner)

    def load(n):
        return pltpu.make_async_copy(source(n, place.core), own.at[n % 2], own_sem.at[n % 2])

    def fetch(n):
        return pltpu.make_async_copy(late_ref.at[n], oth.at[n % 2], oth_sem.at[n % 2])

    def add(dst, *srcs):
        step = 48

        def body(i, _):
            rows = pl.ds(pl.multiple_of(i * step, 16), step)
            total = dst[rows, :]
            for s in srcs:
                total = total + s[rows, :]
            dst[rows, :] = total
            return 0

        lax.fori_loop(0, u // step, body, 0)

    load(0).start()
    load(1).start()
    meet(place)
    for n in range(24):
        exchange(n).start()

    first, second, third = [], [], []
    for n in range(12):
        k = units[n][0]
        load(n).wait()
        exchange(n).wait_recv()
        add(early.at[n], own.at[n % 2])
        load(n + 2).start()
        copy = remote(early.at[n], r1.at[n], s1_send.at[n], s1_recv.at[n], place.flipped(dims_of(k)[0]))
        copy.start()
        first.append(copy)

    for n in range(2):
        exchange(12 + n).wait_recv()
        fetch(n).start()
    for n in range(12):
        k = units[n][0]
        load(12 + n).wait()
        fetch(n).wait()
        first[n].wait_recv()
        add(r1.at[n], own.at[n % 2], oth.at[n % 2])
        if n + 2 < 12:
            load(14 + n).start()
            exchange(14 + n).wait_recv()
            fetch(n + 2).start()
        if n < 6:
            copy = remote(r1.at[n], r2.at[n], s2_send.at[n], s2_recv.at[n], place.flipped(dims_of(k)[1]))
            copy.start()
            second.append(copy)

    for n in range(6):
        second[n].wait_recv()
        add(r1.at[6 + n], r2.at[n])
        if n < 3:
            copy = remote(r1.at[6 + n], r3.at[n], s3_send.at[n], s3_recv.at[n], place.flipped(dims_of(n)[2]))
            copy.start()
            third.append(copy)
    outs = []
    for k in range(3):
        third[k].wait_recv()
        add(r1.at[9 + k], r3.at[k])
        out = pltpu.make_async_copy(r1.at[9 + k], g_ref.at[pl.ds(k * u, u)], out_sem.at[k])
        out.start()
        outs.append(out)
    for out in outs:
        out.wait()
    for n in range(24):
        exchange(n).wait_send()
    for copy in first + second + third:
        copy.wait_send()


def reduce_scatter(plan, f):
    u = plan.unit
    dma = pltpu.SemaphoreType.DMA
    g, _ = pl.pallas_call(
        functools.partial(rs_kernel, plan),
        out_shape=(
            jax.ShapeDtypeStruct((plan.window, LANES), F32),
            jax.ShapeDtypeStruct((12, u, LANES), F32),
        ),
        in_specs=[ANY],
        out_specs=(ANY, ANY),
        scratch_shapes=[pltpu.VMEM((n, u, LANES), F32) for n in (12, 12, 6, 3, 2, 2)]
        + [dma((n,)) for n in (2, 2, 3, 24, 24, 12, 12, 6, 6, 3, 3)],
        compiler_params=pltpu.CompilerParams(
            collective_id=0, has_side_effects=True, vmem_limit_bytes=VMEM_LIMIT
        ),
        name="reduce_scatter",
    )(f)
    return g


def ag_kernel(plan, win, w_ref, own_sem, s_send, s_recv, d_send, d_recv):
    u = plan.unit
    place = Place()
    partner = place.partner()

    def where(k, e):
        row = place.owner(dims_of(k), e, place.core) * plan.window + k * u
        return w_ref.at[pl.ds(pl.multiple_of(row, TILE), u)]

    slot = {(1, 0, 0): 0, (0, 1, 0): 1, (1, 1, 0): 2, (0, 0, 1): 3, (1, 0, 1): 4, (0, 1, 1): 5, (1, 1, 1): 6}

    def src(k, e):
        return win.at[pl.ds(k * u, u)] if e == (0, 0, 0) else where(k, e)

    def send(k, e, n):
        there = list(e)
        there[n] = 1
        s = slot[tuple(there)] * 3 + k
        return remote(src(k, e), where(k, e), s_send.at[s], s_recv.at[s], place.flipped(dims_of(k)[n]))

    def arrival(k, e):
        s = slot[e] * 3 + k
        return remote(where(k, e), where(k, e), s_send.at[s], s_recv.at[s], place.flipped(0))

    def share(k, e):
        s = (slot[e] + 1 if e != (0, 0, 0) else 0) * 3 + k
        return remote(src(k, e), where(k, e), d_send.at[s], d_recv.at[s], partner)

    def shared(k, e):
        s = (slot[e] + 1 if e != (0, 0, 0) else 0) * 3 + k
        row = place.owner(dims_of(k), e, 1 - place.core) * plan.window + k * u
        dst = w_ref.at[pl.ds(pl.multiple_of(row, TILE), u)]
        return remote(dst, dst, d_send.at[s], d_recv.at[s], partner)

    me = place.owner(dims_of(0), (0, 0, 0), place.core) * plan.window
    keep = pltpu.make_async_copy(win, w_ref.at[pl.ds(pl.multiple_of(me, TILE), plan.window)], own_sem)
    meet(place)
    sent = []

    def go(copy):
        copy.start()
        sent.append(copy)

    for n in range(3):
        for k in range(3):
            go(send(k, (0, 0, 0), n))
    keep.start()
    for k in range(3):
        go(share(k, (0, 0, 0)))
    for e in ((1, 0, 0), (0, 1, 0), (0, 0, 1), (1, 1, 0), (1, 0, 1), (0, 1, 1), (1, 1, 1)):
        for k in range(3):
            arrival(k, e).wait_recv()
            for n in range(1, 3):
                if not any(e[n:]):
                    go(send(k, e, n))
            go(share(k, e))
    keep.wait()
    for e in [(0, 0, 0)] + list(slot):
        for k in range(3):
            shared(k, e).wait_recv()
    for copy in sent:
        copy.wait_send()


def all_gather(plan, win):
    dma = pltpu.SemaphoreType.DMA
    return pl.pallas_call(
        functools.partial(ag_kernel, plan),
        out_shape=jax.ShapeDtypeStruct((plan.p * plan.window, LANES), BF),
        in_specs=[pl.BlockSpec(memory_space=pltpu.VMEM)],
        out_specs=ANY,
        scratch_shapes=[dma, dma((21,)), dma((21,)), dma((24,)), dma((24,))],
        compiler_params=pltpu.CompilerParams(collective_id=1, has_side_effects=True),
        name="all_gather",
    )(win)


def restore_kernel(plan, work, depth, w_ref, *refs):
    n = len(plan.big)
    outs, small = refs[:n], refs[n]
    ins, wide, stage = refs[n + 1], refs[n + 2], refs[n + 3:2 * n + 3]
    heads, tails, in_sem, out_sem, edge_sem, small_sem = refs[2 * n + 3:]
    p = plan.p

    def at(tile):
        r = max(r for r in range(p) if plan.first(r) <= tile)
        return r, r * plan.window + (tile - plan.first(r)) * TILE

    def pieces(i):
        _, _, rows, nj, flat = work[i]
        a, b = flat // TILE, (flat + rows * nj) // TILE
        cuts = [a] + [plan.first(r) for r in range(p) if a < plan.first(r) < b] + [b]
        return [(at(lo)[1], (lo - a) * TILE, (hi - lo) * TILE) for lo, hi in zip(cuts, cuts[1:])]

    def loads(i):
        s = i % depth
        return [
            pltpu.make_async_copy(w_ref.at[pl.ds(src, size)], ins.at[s, pl.ds(dst, size)], in_sem.at[s, m])
            for m, (src, dst, size) in enumerate(pieces(i))
        ]

    def store(i):
        k, r, rows, nj, flat = work[i]
        s = i % depth
        return pltpu.make_async_copy(stage[k].at[s], outs[k].at[pl.ds(r, rows)], out_sem.at[s])

    last = plan.first(p - 1)
    off = plan.small_row // TILE - last
    small_copy = pltpu.make_async_copy(
        w_ref.at[pl.ds((p - 1) * plan.window + off * TILE, small.shape[0])], ins.at[depth, pl.ds(0, small.shape[0])],
        small_sem,
    )
    small_copy.start()
    edges = []
    for r in range(1, p):
        t = plan.first(r)
        before = (r - 1) * plan.window + (t - plan.first(r - 1)) * TILE
        edges.append(pltpu.make_async_copy(w_ref.at[pl.ds(r * plan.window, TILE)], heads.at[r], edge_sem.at[0, r]))
        edges.append(pltpu.make_async_copy(w_ref.at[pl.ds(before, TILE)], tails.at[r], edge_sem.at[1, r]))
    for i in range(depth):
        for c in loads(i):
            c.start()
    for c in edges:
        c.start()
    for c in edges:
        c.wait()
    where = lax.broadcasted_iota(jnp.int32, (TILE, LANES), 0) * LANES + lax.broadcasted_iota(jnp.int32, (TILE, LANES), 1)
    for r in range(1, p):
        cut = r * plan.shard - plan.first(r) * TILE * LANES
        merged = jnp.where(where < cut, tails[r].astype(F32), heads[r].astype(F32))
        heads[r] = merged.astype(BF)
    small_copy.wait()
    small_out = pltpu.make_async_copy(ins.at[depth, pl.ds(0, small.shape[0])], small, small_sem)
    small_out.start()

    for i, (k, r, rows, nj, flat) in enumerate(work):
        s = i % depth
        for c in loads(i):
            c.wait()
        a, b = flat // TILE, (flat + rows * nj) // TILE
        for d in range(1, p):
            t = plan.first(d)
            if a <= t < b:
                ins[s, pl.ds((t - a) * TILE, TILE), :] = heads[d]
        if i >= depth:
            store(i - depth).wait()
        step = group_rows(rows, nj)

        def widen(g, _, s=s, size=step * nj):
            rs = pl.ds(pl.multiple_of(g * size, TILE), size)
            wide[rs, :] = ins[s, rs, :].astype(F32)
            return 0

        lax.fori_loop(0, rows // step, widen, 0)

        def body(g, _, k=k, s=s, nj=nj, step=step):
            for h in range(0, step, TILE):
                dst = pl.multiple_of(g * step + h, TILE)
                src = pl.multiple_of(dst * nj, TILE)
                for j in range(nj):
                    x = wide[pl.ds(src + j, TILE, stride=nj), :]
                    stage[k][s, pl.ds(dst, TILE), j * LANES:(j + 1) * LANES] = x.astype(BF)
            return 0

        lax.fori_loop(0, rows // step, body, 0)
        store(i).start()
        if i + depth < len(work):
            for c in loads(i + depth):
                c.start()
    for i in range(len(work) - depth, len(work)):
        store(i).wait()
    small_out.wait()


def restore(plan, wide, shapes):
    n = len(plan.big)
    depth = 3
    work = plan.chunks(3456)
    step = {w[0]: w[2] for w in work}
    size = max(w[2] * w[3] for w in work)
    small_rows = -(-plan.small_size // (LANES * TILE)) * TILE
    dma = pltpu.SemaphoreType.DMA
    outs = pl.pallas_call(
        functools.partial(restore_kernel, plan, work, depth),
        out_shape=[jax.ShapeDtypeStruct((rows, nj * LANES), BF) for rows, nj, _ in plan.big]
        + [jax.ShapeDtypeStruct((small_rows, LANES), BF)],
        in_specs=[ANY],
        out_specs=[ANY] * (n + 1),
        scratch_shapes=[pltpu.VMEM((depth + 1, size, LANES), BF), pltpu.VMEM((size, LANES), F32)]
        + [pltpu.VMEM((depth, step[k], plan.big[k][1] * LANES), BF) for k in range(n)]
        + [pltpu.VMEM((plan.p, TILE, LANES), BF), pltpu.VMEM((plan.p, TILE, LANES), BF)]
        + [dma((depth, 3)), dma((depth,)), dma((2, plan.p)), dma],
        compiler_params=pltpu.CompilerParams(vmem_limit_bytes=VMEM_LIMIT),
        name="restore",
    )(wide)
    flat = outs[n].reshape(-1)
    result = [x.reshape(s) for x, s in zip(outs[:n], shapes)]
    start = 0
    for s in shapes[n:]:
        size = math.prod(s)
        result.append(flat[start:start + size].reshape(s))
        start += size
    return tuple(result)


def adam_update(g, m, v, w, lr, beta1, beta2, eps, step):
    t = step.astype(jnp.float32)
    m_new = beta1 * m + (1.0 - beta1) * g
    v_new = beta2 * v + (1.0 - beta2) * (g * g)
    m_hat = m_new / (1.0 - beta1 ** t)
    v_hat = v_new / (1.0 - beta2 ** t)
    w_new = w - lr * m_hat / (jnp.sqrt(v_hat) + eps)
    return m_new, v_new, w_new


def solution(mesh):
    p = mesh.shape["outer"] * mesh.shape["inner"]

    def body(g_emb, g_qkv, g_o, g_w1, g_w2, g_bqkv, g_b1, g_dvec, m, v, w, lr, beta1, beta2, eps, step):
        grads = (g_emb, g_qkv, g_o, g_w1, g_w2, g_bqkv, g_b1, g_dvec)
        shapes = tuple(x.shape[1:] for x in grads)
        plan = Plan(shapes, p)
        local = flatten(plan, grads)
        total = reduce_scatter(plan, local).reshape(-1)
        r = lax.axis_index(AXES)
        offset = r * plan.shard - plan.first(r) * TILE * LANES
        g = lax.dynamic_slice(total, (offset,), (plan.shard,)) / p
        m_new, v_new, w_new = adam_update(g, m, v, w, lr, beta1, beta2, eps, step)
        win = jnp.zeros((plan.window * LANES,), BF)
        win = lax.dynamic_update_slice(win, w_new.astype(BF), (offset,))
        wb = all_gather(plan, win.reshape(plan.window, LANES))
        return (m_new, v_new, w_new) + restore(plan, wb, shapes)

    g3 = P(AXES, None, None)
    g4 = P(AXES, None, None, None)
    flat = P(AXES)
    rep = P()
    in_specs = (g3, g4, g4, g4, g4, g3, g3, g4, flat, flat, flat, rep, rep, rep, rep, rep)
    out_specs = (flat, flat, flat, rep, rep, rep, rep, rep, rep, rep, rep)
    return jax.shard_map(body, mesh=mesh, in_specs=in_specs, out_specs=out_specs, check_vma=False)
```

time: 1230 us -> 490 us (0.40)
  waiting for transfers between devices: 932 us -> 0 us
  Pallas kernels: 0 us -> 429 us
  local copies, waits for them, and re-layouts: 259 us -> 41.4 us
  between operations: 17.5 us -> 4.07 us
    unnamed x4 -> x0, waiting for transfers between devices: 932 us -> none
    pallas_call x0 -> x4, Pallas kernels: none -> 429 us  [the longest x1 234 us: reduce_scatter(): pl.pallas_call(functools.partial(rs_kernel, plan), out_shape=(jax.ShapeDt...]
    unnamed x41 -> x5, local copies, waits for them, and re-layouts: 113 us -> 3.48 us
    reshape x12 -> x5, local copies, waits for them, and re-layouts: 104 us -> 2.01 us  [the longest x3 1.27 us: restore(): result.append(flat[start:start + size].reshape(s))]
    slice x11 -> x3, local copies, waits for them, and re-layouts: 40.5 us -> 2.16 us  [restore(): result.append(flat[start:start + size].reshape(s))]
    dynamic_update_slice x0 -> x1, local copies, waits for them, and re-layouts: none -> 33.6 us  [body(): win = lax.dynamic_update_slice(win, w_new.astype(BF), (offset,))]
  transfers between devices with their start and end apart: 2 -> 0, of which waited for: 2 -> 0; matrix products, arithmetic and copies ran while one was open for 0% -> 0% of each run, Pallas kernels for 0% -> 0%
where the time goes in v1:
time: 490 us; the launch traced here: 486 us
  Pallas kernels  429 us (88%)
  local copies, waits for them, and re-layouts  41.4 us (8%)
  other arithmetic  11.5 us (2%)
    pallas_call x1, Pallas kernels, reduce_scatter(): pl.pallas_call(functools.partial(rs_kernel, plan), out_shape=(jax.ShapeDt...  234 us
    pallas_call x1, Pallas kernels, all_gather(): pl.pallas_call(functools.partial(ag_kernel, plan), out_shape=jax.ShapeDty...  118 us
    pallas_call x1, Pallas kernels, flatten(): pl.pallas_call(functools.partial(flatten_kernel, plan, work, depth), out_...  45.9 us
    dynamic_update_slice x1, local copies, waits for them, and re-layouts, body(): win = lax.dynamic_update_slice(win, w_new.astype(BF), (offset,))  33.6 us
    pallas_call x1, Pallas kernels, restore(): pl.pallas_call(functools.partial(restore_kernel, plan, work, depth), out_...  31.2 us
    convert_element_type x1, other arithmetic, body(): win = lax.dynamic_update_slice(win, w_new.astype(BF), (offset,))  10.9 us

profile of v1, /device:TPU:0, one launch (start us, length us, event | category | flops | bytes accessed | tf_op | source)
XLA Modules:
  0.0 485.7 jit_solution(9351428989318636964)
XLA Ops:
  4.0 0.8 copy.28
  4.8 0.7 copy.30
  5.5 0.7 reshape.88
  6.2 0.7 fusion.refs_5_
  6.9 45.9 %flatten.1.f_ref = f32[135360,128]{1,0:T(8,128)} custom-call(f32[4096,768]{1,0:T(8,128)} %bitcast.18, f32[1536,2304]{1,0:T(8,128)} %bitcast.17, f32[1536,768]{1,0:T(8,128)} %bitcast.20, f32[1536,3072]{1,0:T(8,128)} %bitcast.15, f32[6144,768]{1,0:T(8,128)} %bitcast.16, f32[192,128]{1,0:T(8,128)} %fusion.refs_5_), custom_call_target="tpu_custom_call" | custom-call | tf_op jit(solution)/shard_map/flatten/pallas_call | solution.py:121
  52.8 233.8 %reduce_scatter.1 = (f32[8496,128]{1,0:T(8,128)}, f32[12,2832,128]{2,1,0:T(8,128)}) custom-call(f32[135360,128]{1,0:T(8,128)} %flatten.1.f_ref), custom_call_target="tpu_custom_call" | custom-call | tf_op jit(solution)/shard_map/reduce_scatter/pallas_call | solution.py:270
  286.6 10.9 %fusion.1 = (bf16[1082592]{0:T(1024)(128)(2,1)}, f32[1082592]{0:T(1024)}, f32[1082592]{0:T(1024)}, f32[1082592]{0:T(1024)}) fusion(f32[1082592]{0:T(1024)} %param.26, f32[]{:T(128)S(6)} %copy.35, f32[]{:T(128)S(6)} %sub.22, f32[]{:T(128)S(6)} %sub.21, f32[]{:T(128)S(6)} %copy.32, f32[1087488]{0:T(1024)} %bitcast.21, s32[]{:T(128)S(6)} %select_n.4, ...), kind=kLoop, calls=%fused_computation.7 | loop fusion | flops 16238880 | bytes 32477796 | tf_op jit(solution)/shard_map/convert_element_type | solution.py:517
  297.5 0.2 broadcast_in_dim.3
  297.7 33.6 %dynamic_update_slice.3 = bf16[1087488]{0:T(1024)(128)(2,1)S(1)} dynamic-update-slice(bf16[1087488]{0:T(1024)(128)(2,1)S(1)} %broadcast_in_dim.3, bf16[1082592]{0:T(1024)(128)(2,1)} %get-tuple-element.47, s32[]{:T(128)S(6)} %select_n.4) | dynamic-update-slice | bytes 4330372 | tf_op jit(solution)/shard_map/dynamic_update_slice | solution.py:517
  331.3 0.0 copy-start
  331.3 1.3 copy-done
  332.6 117.8 %all_gather.1.w_ref = bf16[135936,128]{1,0:T(8,128)(2,1)} custom-call(bf16[8496,128]{1,0:T(8,128)(2,1)} %bitcast.19), custom_call_target="tpu_custom_call" | custom-call | tf_op jit(solution)/shard_map/all_gather/pallas_call | solution.py:354
  450.4 31.2 %restore.1 = (bf16[4096,768]{1,0:T(8,128)(2,1)}, bf16[1536,2304]{1,0:T(8,128)(2,1)}, bf16[1536,768]{1,0:T(8,128)(2,1)}, bf16[1536,3072]{1,0:T(8,128)(2,1)}, bf16...) custom-call(bf16[135936,128]{1,0:T(8,128)(2,1)} %all_gather.1.w_ref), custom_call_target="tpu_custom_call" | custom-call | tf_op jit(solution)/shard_map/restore/pallas_call | solution.py:470
  481.7 0.7 slice.12
  482.4 0.6 reshape.98
  483.0 0.7 slice.13
  483.7 0.6 reshape.99
  484.3 0.7 slice.14
  485.1 0.6 copy.29
  (2 shorter events, 0.0 us)
Async XLA Ops:
  331.3 1.3 copy-start

commit v2 on v0

v2 whole, which is shorter than its diff:
```python
import functools
import math

import jax
import jax.numpy as jnp
from jax import lax
from jax.experimental import pallas as pl
from jax.experimental.pallas import tpu as pltpu
from jax.sharding import PartitionSpec as P

AXES = ("outer", "inner")
MESH = pl.DeviceIdType.MESH
ANY = pl.BlockSpec(memory_space=pl.ANY)
LANES = 128
TILE = 16
VMEM_LIMIT = 63 * 1024 * 1024
BF = jnp.bfloat16
F32 = jnp.float32

ORDER = ((1, 1), (1, 0), (0, 1), (0, 0))


class Plan:
    def __init__(self, shapes, p):
        self.p = p
        self.sizes = [math.prod(s) for s in shapes]
        self.total = sum(self.sizes)
        self.shard = self.total // p
        self.big = []
        start = 0
        for s, n in zip(shapes, self.sizes):
            if s[-2] % TILE == 0:
                self.big.append((n // LANES, s[-1] // LANES, start // LANES))
                start += n
        self.small_row = start // LANES
        self.small_size = self.total - start
        self.starts, need = [], 0
        for r in range(p):
            self.starts.append(self.group(r * self.shard // LANES)[0])
            low, size = self.group(((r + 1) * self.shard - 1) // LANES)
            need = max(need, low + size - self.starts[r])
        self.unit = -(-need // (3 * 48)) * 48
        self.window = 3 * self.unit
        self.small_rows = self.starts[p - 1] + self.window - self.small_row

    def group(self, row):
        for n, nj, flat in self.big:
            if flat <= row < flat + n:
                size = 8 * nj
                return flat + (row - flat) // size * size, size
        return self.small_row + (row - self.small_row) // TILE * TILE, TILE

    def pieces(self, lo, hi):
        spans = [(flat, flat + n) for n, _, flat in self.big]
        spans.append((self.small_row, self.small_row + self.small_rows))
        out = []
        for k, (a, b) in enumerate(spans):
            x, y = max(a, lo), min(b, hi)
            if x < y:
                out.append((k, x - a, y - x, x - lo))
        return out

    def start(self, r):
        row = jnp.int32(self.starts[0])
        for i in range(1, self.p):
            row = jnp.where(r == i, jnp.int32(self.starts[i]), row)
        return row

    def segments(self, first):
        out = []
        for n, nj, flat in self.big:
            lo = jnp.maximum(first, flat)
            hi = jnp.minimum(first + self.window, flat + n)
            out.append((nj, lo - first, lax.div(jnp.maximum(hi - lo, 0), 8 * nj)))
        lo = jnp.maximum(first, self.small_row)
        hi = first + self.window
        out.append((1, lo - first, lax.div(jnp.maximum(hi - lo, 0), TILE)))
        return out


def as_stored(x, nj):
    return x.reshape(-1, 8, nj, LANES).transpose(0, 2, 1, 3).reshape(-1, LANES)


def from_stored(x, nj, shape):
    return x.reshape(-1, nj, 8, LANES).transpose(0, 2, 1, 3).reshape(shape)


class Place:
    def __init__(self):
        o, i = lax.axis_index("outer"), lax.axis_index("inner")
        self.bits = [lax.div(o, 2), lax.rem(o, 2), lax.div(i, 2)]
        self.core = lax.rem(i, 2)

    def flipped(self, d):
        b = list(self.bits)
        b[d] = 1 - b[d]
        return (b[0] * 2 + b[1], b[2] * 2 + self.core)

    def partner(self):
        return (self.bits[0] * 2 + self.bits[1], self.bits[2] * 2 + 1 - self.core)

    def neighbour(self, k, n):
        d = lax.rem(k + n, 3)
        b = [jnp.where(d == i, 1 - x, x) for i, x in enumerate(self.bits)]
        return (b[0] * 2 + b[1], b[2] * 2 + self.core)

    def block(self, n, core):
        k = lax.rem(n, 3)
        a = lax.div(n, 3)
        e = [1 - lax.div(a, 4), 1 - lax.rem(lax.div(a, 2), 2), 1 - lax.rem(a, 2)]
        r = core
        for d, weight in enumerate((8, 4, 2)):
            j = lax.rem(d - k + 3, 3)
            flip = jnp.where(j == 0, e[0], jnp.where(j == 1, e[1], e[2]))
            r = r + weight * (self.bits[d] + flip - 2 * self.bits[d] * flip)
        return r, k

    def owner(self, dims, e, core):
        b = list(self.bits)
        for d, flip in zip(dims, e):
            if flip:
                b[d] = 1 - b[d]
        return b[0] * 8 + b[1] * 4 + b[2] * 2 + core


def dims_of(k):
    return (k, (k + 1) % 3, (k + 2) % 3)


def meet(place):
    barrier = pltpu.get_barrier_semaphore()
    peers = [place.partner()] + [place.flipped(d) for d in range(3)]
    for peer in peers:
        pl.semaphore_signal(barrier, inc=1, device_id=peer, device_id_type=MESH)
    pl.semaphore_wait(barrier, len(peers))


def remote(src, dst, send, recv, dev):
    return pltpu.make_async_remote_copy(
        src_ref=src, dst_ref=dst, send_sem=send, recv_sem=recv, device_id=dev, device_id_type=MESH
    )


def rs_kernel(plan, *refs):
    n_in = len(plan.big) + 1
    xs, g_ref, late_ref = refs[:n_in], refs[n_in], refs[n_in + 1]
    early, r1, r2, r3, own, oth, flat = refs[n_in + 2:n_in + 9]
    (own_sem, oth_sem, out_sem, d_send, d_recv, s1_send, s1_recv, s2_send, s2_recv, s3_send, s3_recv) = refs[n_in + 9:]
    u = plan.unit
    place = Place()
    partner = place.partner()

    def pick(n, core, issue):
        r, k = place.block(n, core)
        for k0 in range(3):

            @pl.when(k == k0)
            def _(k0=k0):
                for r0 in range(plan.p):

                    @pl.when(r == r0)
                    def _(r0=r0):
                        lo = plan.starts[r0] + k0 * u
                        for t, row, size, at in plan.pieces(lo, lo + u):
                            issue(xs[t].at[pl.ds(row, size)], at, size)

    def exchange(i, _):
        def early_out(src, at, size):
            remote(src, early.at[i, pl.ds(at, size)], d_send.at[i], d_recv.at[i], partner).start()

        pick(i, 1 - place.core, early_out)
        return 0

    def exchange_late(i, _):
        def late_out(src, at, size):
            remote(src, late_ref.at[i, pl.ds(at, size)], d_send.at[12 + i], d_recv.at[12 + i], partner).start()

        pick(12 + i, 1 - place.core, late_out)
        return 0

    def arrived(i):
        return remote(early.at[i], early.at[i], d_send.at[i], d_recv.at[i], partner)

    def arrived_late(i):
        return remote(late_ref.at[i], late_ref.at[i], d_send.at[12 + i], d_recv.at[12 + i], partner)

    def load(i):
        slot = lax.rem(i, 2)

        def issue(src, at, size):
            pltpu.make_async_copy(src, own.at[slot, pl.ds(at, size)], own_sem.at[slot]).start()

        pick(i, place.core, issue)

    def loaded(i):
        slot = lax.rem(i, 2)
        return pltpu.make_async_copy(late_ref.at[0], own.at[slot], own_sem.at[slot])

    def fetch(i):
        slot = lax.rem(i, 2)
        return pltpu.make_async_copy(late_ref.at[i], oth.at[slot], oth_sem.at[slot])

    def hop(stage, i):
        src, dst, send, recv = (
            (early, r1, s1_send, s1_recv), (r1, r2, s2_send, s2_recv)
        )[stage]
        return remote(src.at[i], dst.at[i], send.at[i], recv.at[i], place.neighbour(lax.rem(i, 3), stage))

    def last_hop(k):
        return remote(r1.at[6 + k], r3.at[k], s3_send.at[k], s3_recv.at[k], place.flipped(dims_of(k)[2]))

    def add(dst, *srcs):
        step = 48

        def body(i, _):
            rows = pl.ds(pl.multiple_of(i * step, 16), step)
            total = dst[rows, :]
            for s in srcs:
                total = total + s[rows, :]
            dst[rows, :] = total
            return 0

        lax.fori_loop(0, u // step, body, 0)

    def preload(i, _):
        load(i)
        return 0

    meet(place)
    lax.fori_loop(0, 12, exchange, 0)
    lax.fori_loop(0, 2, preload, 0)
    lax.fori_loop(0, 12, exchange_late, 0)

    def first(i, _):
        slot = lax.rem(i, 2)
        loaded(i).wait()
        arrived(i).wait_recv()
        add(early.at[i], own.at[slot])
        hop(0, i).start()
        load(i + 2)
        return 0

    lax.fori_loop(0, 12, first, 0)

    for i in range(2):
        arrived_late(i).wait_recv()
        fetch(i).start()

    def second(i, _):
        slot = lax.rem(i, 2)
        loaded(i).wait()
        fetch(i).wait()
        hop(0, i).wait_recv()
        add(r1.at[i], own.at[slot], oth.at[slot])

        @pl.when(i < 6)
        def _():
            hop(1, i).start()

        @pl.when(i < 10)
        def _():
            load(i + 14)
            arrived_late(i + 2).wait_recv()
            fetch(i + 2).start()

        return 0

    lax.fori_loop(0, 12, second, 0)

    for i in range(6):
        hop(1, i).wait_recv()
        add(r1.at[6 + i], r2.at[i])
        if i < 3:
            last_hop(i).start()
    for k in range(3):
        last_hop(k).wait_recv()
        add(r1.at[9 + k], r3.at[k])
    first_row = plan.start(place.owner(dims_of(0), (0, 0, 0), place.core))
    stored = r1.at[pl.ds(9, 3)].reshape(3 * u, LANES)
    for nj, row, groups in plan.segments(first_row):

        def sort(i, _, nj=nj, row=row):
            size = 8 * nj if nj > 1 else TILE
            base = pl.multiple_of(row + i * size, TILE)
            if nj == 1:
                flat[pl.ds(base, TILE), :] = stored[pl.ds(base, TILE), :]
            else:
                for j in range(nj):
                    flat[pl.ds(base + j, 8, stride=nj), :] = stored[pl.ds(base + j * 8, 8), :]
            return 0

        lax.fori_loop(0, groups, sort, 0)
    out = pltpu.make_async_copy(flat, g_ref, out_sem)
    out.start()

    def sent(i, _):
        arrived(i).wait_send()
        arrived_late(i).wait_send()
        hop(0, i).wait_send()
        return 0

    lax.fori_loop(0, 12, sent, 0)
    for i in range(6):
        hop(1, i).wait_send()
    for k in range(3):
        last_hop(k).wait_send()
    out.wait()


def reduce_scatter(plan, xs):
    u = plan.unit
    dma = pltpu.SemaphoreType.DMA
    g, _ = pl.pallas_call(
        functools.partial(rs_kernel, plan),
        out_shape=(
            jax.ShapeDtypeStruct((plan.window, LANES), F32),
            jax.ShapeDtypeStruct((12, u, LANES), F32),
        ),
        in_specs=[ANY] * len(xs),
        out_specs=(ANY, ANY),
        scratch_shapes=[pltpu.VMEM((n, u, LANES), F32) for n in (12, 12, 6, 3, 2, 2)]
        + [pltpu.VMEM((plan.window, LANES), F32)]
        + [dma((2,)), dma((2,)), dma] + [dma((n,)) for n in (24, 24, 12, 12, 6, 6, 3, 3)],
        compiler_params=pltpu.CompilerParams(
            collective_id=0, has_side_effects=True, vmem_limit_bytes=VMEM_LIMIT
        ),
        name="reduce_scatter",
    )(*xs)
    return g


def ag_kernel(plan, values, w_ref, win, own_sem, s_send, s_recv, d_send, d_recv):
    u = plan.unit
    place = Place()
    partner = place.partner()

    for nj, row, groups in plan.segments(plan.start(place.owner(dims_of(0), (0, 0, 0), place.core))):

        def sort(i, _, nj=nj, row=row):
            size = 8 * nj if nj > 1 else TILE
            base = pl.multiple_of(row + i * size, TILE)
            if nj == 1:
                win[pl.ds(base, TILE), :] = values[pl.ds(base, TILE), :].astype(BF)
            else:
                for j in range(0, nj, 2):
                    pair = [values[pl.ds(base + j + h, 8, stride=nj), :] for h in range(2)]
                    win[pl.ds(base + j * 8, TILE), :] = jnp.concatenate(pair, axis=0).astype(BF)
            return 0

        lax.fori_loop(0, groups, sort, 0)

    def where(k, e):
        row = place.owner(dims_of(k), e, place.core) * plan.window + k * u
        return w_ref.at[pl.ds(pl.multiple_of(row, TILE), u)]

    slot = {(1, 0, 0): 0, (0, 1, 0): 1, (1, 1, 0): 2, (0, 0, 1): 3, (1, 0, 1): 4, (0, 1, 1): 5, (1, 1, 1): 6}

    def src(k, e):
        return win.at[pl.ds(k * u, u)] if e == (0, 0, 0) else where(k, e)

    def send(k, e, n):
        there = list(e)
        there[n] = 1
        s = slot[tuple(there)] * 3 + k
        return remote(src(k, e), where(k, e), s_send.at[s], s_recv.at[s], place.flipped(dims_of(k)[n]))

    def arrival(k, e):
        s = slot[e] * 3 + k
        return remote(where(k, e), where(k, e), s_send.at[s], s_recv.at[s], place.flipped(0))

    def share(k, e):
        s = (slot[e] + 1 if e != (0, 0, 0) else 0) * 3 + k
        return remote(src(k, e), where(k, e), d_send.at[s], d_recv.at[s], partner)

    def shared(k, e):
        s = (slot[e] + 1 if e != (0, 0, 0) else 0) * 3 + k
        row = place.owner(dims_of(k), e, 1 - place.core) * plan.window + k * u
        dst = w_ref.at[pl.ds(pl.multiple_of(row, TILE), u)]
        return remote(dst, dst, d_send.at[s], d_recv.at[s], partner)

    me = place.owner(dims_of(0), (0, 0, 0), place.core) * plan.window
    keep = pltpu.make_async_copy(win, w_ref.at[pl.ds(pl.multiple_of(me, TILE), plan.window)], own_sem)
    meet(place)
    sent = []

    def go(copy):
        copy.start()
        sent.append(copy)

    for n in range(3):
        for k in range(3):
            go(send(k, (0, 0, 0), n))
    keep.start()
    for k in range(3):
        go(share(k, (0, 0, 0)))
    for e in ((1, 0, 0), (0, 1, 0), (0, 0, 1), (1, 1, 0), (1, 0, 1), (0, 1, 1), (1, 1, 1)):
        for k in range(3):
            arrival(k, e).wait_recv()
            for n in range(1, 3):
                if not any(e[n:]):
                    go(send(k, e, n))
            go(share(k, e))
    keep.wait()
    for e in [(0, 0, 0)] + list(slot):
        for k in range(3):
            shared(k, e).wait_recv()
    for copy in sent:
        copy.wait_send()


def all_gather(plan, win):
    dma = pltpu.SemaphoreType.DMA
    return pl.pallas_call(
        functools.partial(ag_kernel, plan),
        out_shape=jax.ShapeDtypeStruct((plan.p * plan.window, LANES), BF),
        in_specs=[pl.BlockSpec(memory_space=pltpu.VMEM)],
        out_specs=ANY,
        scratch_shapes=[pltpu.VMEM((plan.window, LANES), BF), dma, dma((21,)), dma((21,)), dma((24,)), dma((24,))],
        compiler_params=pltpu.CompilerParams(collective_id=1, has_side_effects=True, vmem_limit_bytes=16 * 1024 * 1024),
        name="all_gather",
    )(win)


def restore_kernel(plan, work, depth, w_ref, *refs):
    n = len(plan.big) + 1
    outs = refs[:n]
    buf, heads, tails, in_sem, out_sem, edge_sem = refs[n:]
    p, ahead = plan.p, depth // 2

    def parts(i):
        _, _, rows, flat = work[i]
        cuts = [flat] + [s for s in plan.starts[1:] if flat < s < flat + rows] + [flat + rows]
        out = []
        for lo, hi in zip(cuts, cuts[1:]):
            r = max(r for r in range(p) if plan.starts[r] <= lo)
            out.append((r * plan.window + lo - plan.starts[r], lo - flat, hi - lo))
        return out

    def loads(i):
        s = i % depth
        return [
            pltpu.make_async_copy(w_ref.at[pl.ds(src, size)], buf.at[s, pl.ds(dst, size)], in_sem.at[s, m])
            for m, (src, dst, size) in enumerate(parts(i))
        ]

    def store(i):
        k, row, rows, _ = work[i]
        s = i % depth
        return pltpu.make_async_copy(buf.at[s, pl.ds(0, rows)], outs[k].at[pl.ds(row, rows)], out_sem.at[s])

    edges, size = [], [0] * p
    for r in range(1, p):
        size[r] = plan.group(plan.starts[r])[1]
        before = (r - 1) * plan.window + plan.starts[r] - plan.starts[r - 1]
        for m, (ref, src) in enumerate(((heads, r * plan.window), (tails, before))):
            edges.append(
                pltpu.make_async_copy(w_ref.at[pl.ds(src, size[r])], ref.at[r, pl.ds(0, size[r])], edge_sem.at[m, r])
            )
    for c in edges:
        c.start()
    for i in range(ahead):
        for c in loads(i):
            c.start()
    for c in edges:
        c.wait()
    for r in range(1, p):
        nj = size[r] // 8
        shape = (size[r], LANES)
        row, lane = lax.broadcasted_iota(jnp.int32, shape, 0), lax.broadcasted_iota(jnp.int32, shape, 1)
        at = (lax.rem(row, 8) * nj + lax.div(row, 8)) * LANES + lane
        cut = r * plan.shard - plan.starts[r] * LANES
        rows = pl.ds(0, size[r])
        heads[r, rows, :] = jnp.where(at < cut, tails[r, rows, :].astype(F32), heads[r, rows, :].astype(F32)).astype(BF)

    for i, (k, row, rows, flat) in enumerate(work):
        s = i % depth
        for c in loads(i):
            c.wait()
        for r in range(1, p):
            if flat <= plan.starts[r] < flat + rows:
                buf[s, pl.ds(plan.starts[r] - flat, size[r]), :] = heads[r, pl.ds(0, size[r]), :]
        store(i).start()
        if i + ahead < len(work):
            if i + ahead >= depth:
                store(i + ahead - depth).wait()
            for c in loads(i + ahead):
                c.start()
    for i in range(max(0, len(work) - depth), len(work)):
        store(i).wait()


def restore(plan, gathered, shapes):
    n = len(plan.big)
    depth, top = 8, 192
    work = []
    for k, (rows, nj, flat) in enumerate(plan.big):
        step = max(c for c in range(8 * nj, 3457, 8 * nj) if rows % c == 0)
        work += [(k, r, step, flat + r) for r in range(0, rows, step)]
    small_rows = -(-plan.small_size // (LANES * TILE)) * TILE
    work.append((n, 0, small_rows, plan.small_row))
    dma = pltpu.SemaphoreType.DMA
    outs = pl.pallas_call(
        functools.partial(restore_kernel, plan, work, depth),
        out_shape=[jax.ShapeDtypeStruct((rows, LANES), BF) for rows, _, _ in plan.big]
        + [jax.ShapeDtypeStruct((small_rows, LANES), BF)],
        in_specs=[ANY],
        out_specs=[ANY] * (n + 1),
        scratch_shapes=[pltpu.VMEM((depth, max(w[2] for w in work), LANES), BF)]
        + [pltpu.VMEM((plan.p, top, LANES), BF)] * 2
        + [dma((depth, 3)), dma((depth,)), dma((2, plan.p))],
        compiler_params=pltpu.CompilerParams(vmem_limit_bytes=32 * 1024 * 1024),
        name="restore",
    )(gathered)
    flat = outs[n].reshape(-1)
    result = [from_stored(x, nj, s) for x, (_, nj, _), s in zip(outs, plan.big, shapes)]
    start = 0
    for s in shapes[n:]:
        size = math.prod(s)
        result.append(flat[start:start + size].reshape(s))
        start += size
    return tuple(result)


def adam_update(g, m, v, w, lr, beta1, beta2, eps, step):
    t = step.astype(jnp.float32)
    m_new = beta1 * m + (1.0 - beta1) * g
    v_new = beta2 * v + (1.0 - beta2) * (g * g)
    m_hat = m_new / (1.0 - beta1 ** t)
    v_hat = v_new / (1.0 - beta2 ** t)
    w_new = w - lr * m_hat / (jnp.sqrt(v_hat) + eps)
    return m_new, v_new, w_new


def solution(mesh):
    p = mesh.shape["outer"] * mesh.shape["inner"]

    def body(g_emb, g_qkv, g_o, g_w1, g_w2, g_bqkv, g_b1, g_dvec, m, v, w, lr, beta1, beta2, eps, step):
        grads = (g_emb, g_qkv, g_o, g_w1, g_w2, g_bqkv, g_b1, g_dvec)
        shapes = tuple(x.shape[1:] for x in grads)
        plan = Plan(shapes, p)
        n = len(plan.big)
        small = jnp.concatenate([x.reshape(-1) for x in grads[n:]])
        small = jnp.pad(small, (0, plan.small_rows * LANES - plan.small_size)).reshape(-1, LANES)
        stored = [as_stored(x, nj) for x, (_, nj, _) in zip(grads, plan.big)]
        total = reduce_scatter(plan, stored + [small]).reshape(-1)
        r = lax.axis_index(AXES)
        offset = r * plan.shard - plan.start(r) * LANES
        g = lax.dynamic_slice(total, (offset,), (plan.shard,)) / p
        m_new, v_new, w_new = adam_update(g, m, v, w, lr, beta1, beta2, eps, step)
        front = max(i * plan.shard - plan.starts[i] * LANES for i in range(p))
        back = plan.window * LANES - plan.shard
        win = lax.dynamic_slice(jnp.pad(w_new, (front, back)), (front - offset,), (plan.window * LANES,))
        wb = all_gather(plan, win.reshape(plan.window, LANES))
        return (m_new, v_new, w_new) + restore(plan, wb, shapes)

    g3 = P(AXES, None, None)
    g4 = P(AXES, None, None, None)
    flat = P(AXES)
    rep = P()
    in_specs = (g3, g4, g4, g4, g4, g3, g3, g4, flat, flat, flat, rep, rep, rep, rep, rep)
    out_specs = (flat, flat, flat, rep, rep, rep, rep, rep, rep, rep, rep)
    return jax.shard_map(body, mesh=mesh, in_specs=in_specs, out_specs=out_specs, check_vma=False)
```

time: 1230 us -> 406 us (0.33)
  waiting for transfers between devices: 932 us -> 0 us
  Pallas kernels: 0 us -> 384 us
  local copies, waits for them, and re-layouts: 259 us -> 6.22 us
  between operations: 17.5 us -> 4.11 us
    unnamed x4 -> x0, waiting for transfers between devices: 932 us -> none
    pallas_call x0 -> x3, Pallas kernels: none -> 384 us  [the longest x1 239 us: reduce_scatter(): pl.pallas_call(functools.partial(rs_kernel, plan), out_shape=(jax.ShapeDt...]
    unnamed x41 -> x5, local copies, waits for them, and re-layouts: 113 us -> 2.7 us
    reshape x12 -> x6, local copies, waits for them, and re-layouts: 104 us -> 3.49 us  [the longest x1 1.48 us: body(): wb = all_gather(plan, win.reshape(plan.window, LANES))]
    slice x11 -> x3, local copies, waits for them, and re-layouts: 40.5 us -> 0.02 us  [restore(): result.append(flat[start:start + size].reshape(s))]
  transfers between devices with their start and end apart: 2 -> 0, of which waited for: 2 -> 0; matrix products, arithmetic and copies ran while one was open for 0% -> 0% of each run, Pallas kernels for 0% -> 0%
where the time goes in v2:
time: 406 us; the launch traced here: 405 us
  Pallas kernels  384 us (95%)
  other arithmetic  10.7 us (3%)
  local copies, waits for them, and re-layouts  6.22 us (2%)
  between operations  4.11 us (1%)
    pallas_call x1, Pallas kernels, reduce_scatter(): pl.pallas_call(functools.partial(rs_kernel, plan), out_shape=(jax.ShapeDt...  239 us
    pallas_call x1, Pallas kernels, all_gather(): pl.pallas_call(functools.partial(ag_kernel, plan), out_shape=jax.ShapeDty...  120 us
    pallas_call x1, Pallas kernels, restore(): pl.pallas_call(functools.partial(restore_kernel, plan, work, depth), out_...  25 us
    sub x1, other arithmetic, adam_update(): w_new = w - lr * m_hat / (jnp.sqrt(v_hat) + eps)  9.98 us

profile of v2, /device:TPU:0, one launch (start us, length us, event | category | flops | bytes accessed | tf_op | source)
XLA Modules:
  0.0 405.1 jit_solution(6449258352180567694)
XLA Ops:
  4.1 0.7 reshape.126
  4.8 0.7 copy.30
  5.5 0.8 copy.28
  6.3 0.7 fusion.1.refs_5_
  7.0 239.2 %reduce_scatter.1 = (f32[8640,128]{1,0:T(8,128)}, f32[12,2880,128]{2,1,0:T(8,128)}) custom-call(f32[24576,128]{1,0:T(8,128)} %bitcast.60, f32[27648,128]{1,0:T(8,128)} %bitcast.59, f32[9216,128]{1,0:T(8,128)} %bitcast.61, f32[36864,128]{1,0:T(8,128)} %bitcast.57, f32[36864,128]{1,0:T(8,128)} %bitcast.58, f32[336,128]{1,0:T(8,128)} %fusion.1.refs_5_), custom_call_target="tpu_custom_call" | custom-call | tf_op jit(solution)/shard_map/reduce_scatter/pallas_call | solution.py:314
  246.2 10.0 %divide_subtract_fusion = (f32[1082592]{0:T(1024)S(1)}, f32[1082592]{0:T(1024)}, f32[1082592]{0:T(1024)}) fusion(f32[1082592]{0:T(1024)} %param.26, f32[]{:T(128)S(6)} %copy.34, f32[]{:T(128)S(6)} %sub.25, f32[]{:T(128)S(6)} %sub.24, f32[]{:T(128)S(6)} %copy.31, f32[1105920]{0:T(1024)} %bitcast.62, s32[]{:T(128)S(6)} %select_n.67, f32[]{:T(128)S(6)} %sub.23, ...), kind=kLoop, calls=%fused_computation.2 | loop fusion | flops 15156288 | bytes 30312612 | tf_op jit(solution)/shard_map/sub | solution.py:531
  256.2 0.0 copy-start
  256.2 1.5 fusion.values
  257.7 0.6 copy-done
  258.2 120.0 %all_gather.1.w_ref = bf16[138240,128]{1,0:T(8,128)(2,1)} custom-call(f32[8640,128]{1,0:T(8,128)S(1)} %fusion.values), custom_call_target="tpu_custom_call" | custom-call | tf_op jit(solution)/shard_map/all_gather/pallas_call | solution.py:414
  378.2 25.0 %restore.1 = (bf16[24576,128]{1,0:T(8,128)(2,1)}, bf16[27648,128]{1,0:T(8,128)(2,1)}, bf16[9216,128]{1,0:T(8,128)(2,1)}, bf16[36864,128]{1,0:T(8,128)(2,1)}, bf1...) custom-call(bf16[138240,128]{1,0:T(8,128)(2,1)} %all_gather.1.w_ref), custom_call_target="tpu_custom_call" | custom-call | tf_op jit(solution)/shard_map/restore/pallas_call | solution.py:503
  403.2 0.6 reshape.142
  403.8 0.6 reshape.143
  404.5 0.6 copy.29
  (5 shorter events, 0.1 us)
Async XLA Ops:
  256.2 2.1 copy-start

commit v3 on v0

v3 whole, which is shorter than its diff:
```python
import functools
import math

import jax
import jax.numpy as jnp
from jax import lax
from jax.experimental import pallas as pl
from jax.experimental.pallas import tpu as pltpu
from jax.sharding import PartitionSpec as P

AXES = ("outer", "inner")
MESH = pl.DeviceIdType.MESH
ANY = pl.BlockSpec(memory_space=pl.ANY)
LANES = 128
TILE = 16
SPLIT = 4
DEEP = 4
LEAD = 12
BF = jnp.bfloat16
F32 = jnp.float32


class Plan:
    def __init__(self, shapes, p):
        self.p = p
        self.sizes = [math.prod(s) for s in shapes]
        self.total = sum(self.sizes)
        self.shard = self.total // p
        self.big = []
        start = 0
        for s, n in zip(shapes, self.sizes):
            if s[-2] % TILE == 0:
                self.big.append((n // LANES, s[-1] // LANES, start // LANES))
                start += n
        self.small_row = start // LANES
        self.small_size = self.total - start
        self.starts, need = [], 0
        for r in range(p):
            self.starts.append(self.group(r * self.shard // LANES)[0])
            low, size = self.group(((r + 1) * self.shard - 1) // LANES)
            need = max(need, low + size - self.starts[r])
        self.part = -(-need // (3 * SPLIT * TILE)) * TILE
        self.unit = SPLIT * self.part
        self.window = 3 * self.unit
        self.small_rows = self.starts[p - 1] + self.window - self.small_row

    def group(self, row):
        for n, nj, flat in self.big:
            if flat <= row < flat + n:
                size = 8 * nj
                return flat + (row - flat) // size * size, size
        return self.small_row + (row - self.small_row) // TILE * TILE, TILE

    def spans(self):
        spans = [(flat, flat + n) for n, _, flat in self.big]
        return spans + [(self.small_row, self.small_row + self.small_rows)]

    def crossing(self):
        out = {}
        for start in self.starts:
            for lo in range(start, start + self.window, self.part):
                cuts = []
                for t, (x, y) in enumerate(self.spans()):
                    x, y = max(x, lo), min(y, lo + self.part)
                    if x < y:
                        cuts.append((t, x - self.spans()[t][0], y - x, x - lo))
                if len(cuts) > 1:
                    out[lo] = cuts
        return out

    def start(self, r):
        row = jnp.int32(self.starts[0])
        for i in range(1, self.p):
            row = jnp.where(r == i, jnp.int32(self.starts[i]), row)
        return row

    def segments(self, first):
        out = []
        for n, nj, flat in self.big:
            lo = jnp.maximum(first, flat)
            hi = jnp.minimum(first + self.window, flat + n)
            out.append((nj, lo - first, lax.div(jnp.maximum(hi - lo, 0), 8 * nj)))
        return out

    def pairs(self):
        out, row = [], 0
        for n in self.sizes[len(self.big):]:
            out.append((row, n // (2 * LANES)))
            row += n // LANES
        return out


def as_stored(x, nj):
    return x.reshape(-1, 8, nj, LANES).transpose(0, 2, 1, 3).reshape(-1, LANES)


def from_stored(x, nj, shape):
    return x.reshape(-1, nj, 8, LANES).transpose(0, 2, 1, 3).reshape(shape)


class Place:
    def __init__(self):
        o, i = lax.axis_index("outer"), lax.axis_index("inner")
        self.bits = [lax.div(o, 2), lax.rem(o, 2), lax.div(i, 2)]
        self.core = lax.rem(i, 2)

    def flipped(self, d):
        b = list(self.bits)
        b[d] = 1 - b[d]
        return (b[0] * 2 + b[1], b[2] * 2 + self.core)

    def partner(self):
        return (self.bits[0] * 2 + self.bits[1], self.bits[2] * 2 + 1 - self.core)

    def neighbour(self, k, n):
        d = lax.rem(k + n, 3)
        b = [jnp.where(d == i, 1 - x, x) for i, x in enumerate(self.bits)]
        return (b[0] * 2 + b[1], b[2] * 2 + self.core)

    def part(self, i):
        a, s, k = lax.div(i, 3 * SPLIT), lax.rem(lax.div(i, 3), SPLIT), lax.rem(i, 3)
        return a, k, s, a * (3 * SPLIT) + k * SPLIT + s

    def block(self, a, k, core):
        e = [1 - lax.div(a, 4), 1 - lax.rem(lax.div(a, 2), 2), 1 - lax.rem(a, 2)]
        r = core
        for d, weight in enumerate((8, 4, 2)):
            j = lax.rem(d - k + 3, 3)
            flip = jnp.where(j == 0, e[0], jnp.where(j == 1, e[1], e[2]))
            r = r + weight * (self.bits[d] + flip - 2 * self.bits[d] * flip)
        return r

    def owner(self, dims, e, core):
        b = list(self.bits)
        for d, flip in zip(dims, e):
            if flip:
                b[d] = 1 - b[d]
        return b[0] * 8 + b[1] * 4 + b[2] * 2 + core


def dims_of(k):
    return (k, (k + 1) % 3, (k + 2) % 3)


def arrive(place):
    barrier = pltpu.get_barrier_semaphore()
    for peer in [place.partner()] + [place.flipped(d) for d in range(3)]:
        pl.semaphore_signal(barrier, inc=1, device_id=peer, device_id_type=MESH)


def meet():
    pl.semaphore_wait(pltpu.get_barrier_semaphore(), 4)


def remote(src, dst, send, recv, dev):
    return pltpu.make_async_remote_copy(
        src_ref=src, dst_ref=dst, send_sem=send, recv_sem=recv, device_id=dev, device_id_type=MESH
    )


def rs_kernel(plan, *refs):
    n_in = len(plan.big) + 1
    xs, flat, late_ref = refs[:n_in], refs[n_in], refs[n_in + 1]
    early, r1, r2, r3, own, oth = refs[n_in + 2:n_in + 8]
    own_sem, oth_sem, d_send, d_recv, s1_send, s1_recv, s2_send, s2_recv, s3_send, s3_recv = refs[n_in + 8:]
    part = plan.part
    wave = 3 * SPLIT
    early_n = 4 * wave
    place = Place()
    partner = place.partner()
    crossing = plan.crossing()

    def pick(i, core, issue):
        a, k, s, _ = place.part(i)
        row = plan.start(place.block(a, k, core)) + k * plan.unit + s * part
        for t, (lo, hi) in enumerate(plan.spans()):

            @pl.when((row >= lo) & (row <= hi - part))
            def _(t=t, lo=lo):
                issue(xs[t].at[pl.ds(pl.multiple_of(row - lo, TILE), part)], 0, part)

        for first, cuts in crossing.items():

            @pl.when(row == first)
            def _(cuts=cuts):
                for t, at, size, to in cuts:
                    issue(xs[t].at[pl.ds(at, size)], to, size)

    def swap(i):
        slot = place.part(i)[3]

        def issue(src, at, size):
            remote(src, early.at[slot, pl.ds(at, size)], d_send.at[slot], d_recv.at[slot], partner).start()

        pick(i, 1 - place.core, issue)

    def swap_late(i):
        slot = place.part(i)[3]

        def issue(src, at, size):
            remote(
                src, late_ref.at[slot, pl.ds(at, size)], d_send.at[early_n + slot], d_recv.at[early_n + slot], partner
            ).start()

        pick(early_n + i, 1 - place.core, issue)

    def swapped(slot):
        return remote(early.at[slot], early.at[slot], d_send.at[slot], d_recv.at[slot], partner)

    def swapped_late(slot):
        sems = d_send.at[early_n + slot], d_recv.at[early_n + slot]
        return remote(late_ref.at[slot], late_ref.at[slot], *sems, partner)

    def load(i):
        to = lax.rem(i, DEEP)

        def issue(src, at, size):
            pltpu.make_async_copy(src, own.at[to, pl.ds(at, size)], own_sem.at[to]).start()

        pick(i, place.core, issue)

    def loaded(i):
        to = lax.rem(i, DEEP)
        return pltpu.make_async_copy(late_ref.at[0], own.at[to], own_sem.at[to])

    def fetch(i):
        to = lax.rem(i, DEEP)
        return pltpu.make_async_copy(late_ref.at[place.part(i)[3]], oth.at[to], oth_sem.at[to])

    def hop(stage, k, slot):
        src, dst, send, recv, base = (
            (early, r1, s1_send, s1_recv, 0),
            (r1, r2, s2_send, s2_recv, 0),
            (r1, r3, s3_send, s3_recv, 2 * wave),
        )[stage]
        return remote(src.at[base + slot], dst.at[slot], send.at[slot], recv.at[slot], place.neighbour(k, stage))

    def add(dst, *srcs):
        step = 48

        def body(i, _):
            rows = pl.ds(pl.multiple_of(i * step, TILE), step)
            total = dst[rows, :]
            for s in srcs:
                total = total + s[rows, :]
            dst[rows, :] = total
            return 0

        lax.fori_loop(0, part // step, body, 0)

    def loop(count, f):
        def body(i, _):
            f(i)
            return 0

        lax.fori_loop(0, count, body, 0)

    arrive(place)
    loop(DEEP, load)
    meet()
    loop(LEAD, swap)

    def first(i):
        _, k, _, slot = place.part(i)

        @pl.when(i + LEAD < early_n)
        def _():
            swap(i + LEAD)

        @pl.when(i + LEAD >= early_n)
        def _():
            swap_late(i + LEAD - early_n)

        loaded(i).wait()
        swapped(slot).wait_recv()
        add(early.at[slot], own.at[lax.rem(i, DEEP)])
        hop(0, k, slot).start()
        load(i + DEEP)

    loop(early_n, first)

    def prefetch(i):
        swapped_late(place.part(i)[3]).wait_recv()
        fetch(i).start()

    loop(DEEP, prefetch)

    def second(i):
        _, k, _, slot = place.part(i)

        @pl.when(i + LEAD < early_n)
        def _():
            swap_late(i + LEAD)

        to = lax.rem(i, DEEP)
        loaded(i).wait()
        fetch(i).wait()
        hop(0, k, slot).wait_recv()
        add(r1.at[slot], own.at[to], oth.at[to])

        @pl.when(i < 2 * wave)
        def _():
            hop(1, k, slot).start()

        @pl.when(i + DEEP < early_n)
        def _():
            load(early_n + i + DEEP)
            prefetch(i + DEEP)

    loop(early_n, second)

    def third(i):
        _, k, _, slot = place.part(i)
        hop(1, k, slot).wait_recv()
        add(r1.at[2 * wave + slot], r2.at[slot])

        @pl.when(i < wave)
        def _():
            hop(2, k, slot).start()

    loop(2 * wave, third)

    def fourth(i):
        _, k, _, slot = place.part(i)
        hop(2, k, slot).wait_recv()
        add(r1.at[3 * wave + slot], r3.at[slot])

    loop(wave, fourth)

    me = place.owner(dims_of(0), (0, 0, 0), place.core)
    stored = r1.at[pl.ds(3 * wave, wave)].reshape(plan.window, LANES)
    for nj, row, groups in plan.segments(plan.start(me)):

        def sort(i, nj=nj, row=row):
            base = pl.multiple_of(row + i * 8 * nj, TILE)
            for j in range(nj):
                flat[pl.ds(base + j, 8, stride=nj), :] = stored[pl.ds(base + j * 8, 8), :]

        loop(groups, sort)

    @pl.when(me == plan.p - 1)
    def _():
        base = plan.small_row - plan.starts[plan.p - 1]
        for row, nj in plan.pairs():
            for layer in range(2):
                at = base + row + layer * nj
                flat[pl.ds(at, nj), :] = stored[pl.ds(base + row + layer, nj, stride=2), :]

    def sent(i):
        _, k, _, slot = place.part(i)
        swapped(slot).wait_send()
        swapped_late(slot).wait_send()
        hop(0, k, slot).wait_send()

        @pl.when(i < 2 * wave)
        def _():
            hop(1, k, slot).wait_send()

        @pl.when(i < wave)
        def _():
            hop(2, k, slot).wait_send()

    loop(early_n, sent)


def reduce_scatter(plan, xs):
    dma = pltpu.SemaphoreType.DMA
    wave = 3 * SPLIT
    slots = [4 * wave, 4 * wave, 2 * wave, wave, DEEP, DEEP]
    used = (sum(slots) * plan.part * LANES * 4 >> 20) + 2
    g, _ = pl.pallas_call(
        functools.partial(rs_kernel, plan),
        out_shape=(
            pltpu.VMEM((plan.window, LANES), F32),
            jax.ShapeDtypeStruct((4 * wave, plan.part, LANES), F32),
        ),
        in_specs=[ANY] * len(xs),
        out_specs=(pl.BlockSpec(memory_space=pltpu.VMEM), ANY),
        scratch_shapes=[pltpu.VMEM((n, plan.part, LANES), F32) for n in slots]
        + [dma((DEEP,)), dma((DEEP,))]
        + [dma((n * wave,)) for n in (8, 8, 4, 4, 2, 2, 1, 1)],
        compiler_params=pltpu.CompilerParams(
            collective_id=0, has_side_effects=True, vmem_limit_bytes=used << 20
        ),
        name="reduce_scatter",
    )(*xs)
    return g


def ag_kernel(plan, values, *refs):
    w_refs, (win, tiny, s_send, s_recv, d_send, d_recv) = refs[:3], refs[3:]
    part, unit = plan.part, plan.unit
    place = Place()
    partner = place.partner()
    here = (0, 0, 0)
    me = place.owner(dims_of(0), here, place.core)
    arrive(place)

    for nj, row, groups in plan.segments(plan.start(me)):

        def sort(i, _, nj=nj, row=row):
            base = pl.multiple_of(row + i * 8 * nj, TILE)
            for j in range(0, nj, 2):
                pair = [values[pl.ds(base + j + h, 8, stride=nj), :] for h in range(2)]
                win[pl.ds(base + j * 8, TILE), :] = jnp.concatenate(pair, axis=0).astype(BF)
            return 0

        lax.fori_loop(0, groups, sort, 0)

    @pl.when(me == plan.p - 1)
    def _():
        base = plan.small_row - plan.starts[plan.p - 1]
        tiny[...] = jnp.zeros_like(tiny)
        for row, nj in plan.pairs():
            for layer in range(2):
                tiny[pl.ds(row + layer, nj, stride=2), :] = values[pl.ds(base + row + layer * nj, nj), :]
        win[pl.ds(base, tiny.shape[0]), :] = tiny[...].astype(BF)

    def rows_of(k, e, s, core):
        row = place.owner(dims_of(k), e, core) * unit + s * part
        return w_refs[k].at[pl.ds(pl.multiple_of(row, TILE), part)]

    slot = {here: 0, (1, 0, 0): 1, (0, 1, 0): 2, (0, 0, 1): 3, (1, 1, 0): 4, (1, 0, 1): 5, (0, 1, 1): 6, (1, 1, 1): 7}

    def index(k, e, s):
        return (slot[e] * 3 + k) * SPLIT + s

    def src(k, e, s):
        return win.at[pl.ds(k * plan.unit + s * part, part)] if e == here else rows_of(k, e, s, place.core)

    sent = []

    def send(k, e, s, n):
        there = list(e)
        there[n] = 1
        i = index(k, tuple(there), s)
        copy = remote(
            src(k, e, s), rows_of(k, e, s, place.core), s_send.at[i], s_recv.at[i], place.flipped(dims_of(k)[n])
        )
        copy.start()
        sent.append(copy)

    def share(k, e, s):
        i = index(k, e, s)
        copy = remote(src(k, e, s), rows_of(k, e, s, place.core), d_send.at[i], d_recv.at[i], partner)
        copy.start()
        sent.append(copy)

    def arrival(k, e, s):
        i, dst = index(k, e, s), rows_of(k, e, s, place.core)
        return remote(dst, dst, s_send.at[i], s_recv.at[i], partner)

    def shared(k, e, s):
        i, dst = index(k, e, s), rows_of(k, e, s, 1 - place.core)
        return remote(dst, dst, d_send.at[i], d_recv.at[i], partner)

    meet()
    for n in range(3):
        for s in range(SPLIT):
            for k in range(3):
                send(k, here, s, n)
    for s in range(SPLIT):
        for k in range(3):
            share(k, here, s)
    rows = 3 * TILE
    for k in range(3):

        def keep(i, _, k=k):
            at = pl.multiple_of(i * rows, rows)
            w_refs[k][pl.ds(pl.multiple_of(me * unit + at, TILE), rows), :] = win[pl.ds(k * unit + at, rows), :]
            return 0

        lax.fori_loop(0, unit // rows, keep, 0)
    for e in list(slot)[1:]:
        for s in range(SPLIT):
            for k in range(3):
                arrival(k, e, s).wait_recv()
                for n in range(1, 3):
                    if not any(e[n:]):
                        send(k, e, s, n)
                share(k, e, s)
    for e in slot:
        for s in range(SPLIT):
            for k in range(3):
                shared(k, e, s).wait_recv()
    for copy in sent:
        copy.wait_send()

    for r in range(1, plan.p):
        size = plan.group(plan.starts[r])[1]
        nj, shape = size // 8, (size, LANES)
        row, lane = lax.broadcasted_iota(jnp.int32, shape, 0), lax.broadcasted_iota(jnp.int32, shape, 1)
        at = (lax.rem(row, 8) * nj + lax.div(row, 8)) * LANES + lane
        cut = r * plan.shard - plan.starts[r] * LANES
        gap = plan.starts[r] - plan.starts[r - 1] - 2 * unit
        before = w_refs[2][pl.ds((r - 1) * unit + gap, size), :]
        rows = pl.ds(r * unit, size)
        w_refs[0][rows, :] = jnp.where(at < cut, before.astype(F32), w_refs[0][rows, :].astype(F32)).astype(BF)


def all_gather(plan, win):
    dma = pltpu.SemaphoreType.DMA
    n = 8 * 3 * SPLIT
    return pl.pallas_call(
        functools.partial(ag_kernel, plan),
        out_shape=[pltpu.VMEM((plan.p * plan.unit, LANES), BF)] * 3,
        in_specs=[pl.BlockSpec(memory_space=pltpu.VMEM)],
        out_specs=[pl.BlockSpec(memory_space=pltpu.VMEM)] * 3,
        scratch_shapes=[pltpu.VMEM((plan.window, LANES), BF), pltpu.VMEM((small_rows(plan), LANES), F32)]
        + [dma((n,))] * 4,
        compiler_params=pltpu.CompilerParams(collective_id=1, has_side_effects=True, vmem_limit_bytes=8 << 20),
        name="all_gather",
    )(win)


def small_rows(plan):
    return -(-plan.small_size // (LANES * TILE)) * TILE


def restore_kernel(plan, *refs):
    w_refs, outs, out_sem = refs[:3], refs[3:-1], refs[-1]
    p = plan.p
    spans = plan.spans()[:-1] + [(plan.small_row, plan.small_row + small_rows(plan))]
    copies = []
    for r in range(p):
        lo = plan.starts[r]
        hi = plan.starts[r + 1] if r + 1 < p else spans[-1][1]
        for k in range(3):
            first = lo + k * plan.unit
            for t, (x, y) in enumerate(spans):
                x, y = max(x, first), min(y, hi, first + plan.unit)
                if x < y:
                    src = w_refs[k].at[pl.ds(r * plan.unit + x - first, y - x)]
                    dst = outs[t].at[pl.ds(x - spans[t][0], y - x)]
                    copies.append(pltpu.make_async_copy(src, dst, out_sem.at[len(copies)]))
    for c in copies:
        c.start()
    for c in copies:
        c.wait()


def restore(plan, gathered, shapes):
    n = len(plan.big)
    dma = pltpu.SemaphoreType.DMA
    outs = pl.pallas_call(
        functools.partial(restore_kernel, plan),
        out_shape=[jax.ShapeDtypeStruct((rows, LANES), BF) for rows, _, _ in plan.big]
        + [jax.ShapeDtypeStruct((small_rows(plan), LANES), BF)],
        in_specs=[ANY] * 3,
        out_specs=[ANY] * (n + 1),
        scratch_shapes=[dma((3 * plan.p + n + 1,))],
        compiler_params=pltpu.CompilerParams(vmem_limit_bytes=1 << 20),
        name="restore",
    )(*gathered)
    result = [from_stored(x, nj, s) for x, (_, nj, _), s in zip(outs, plan.big, shapes)]
    small = outs[n].reshape(-1, 2, LANES)
    for (row, nj), s in zip(plan.pairs(), shapes[n:]):
        result.append(small[row // 2:row // 2 + nj].transpose(1, 0, 2).reshape(s))
    return tuple(result)


def adam_update(g, m, v, w, lr, beta1, beta2, eps, step):
    t = step.astype(jnp.float32)
    m_new = beta1 * m + (1.0 - beta1) * g
    v_new = beta2 * v + (1.0 - beta2) * (g * g)
    m_hat = m_new / (1.0 - beta1 ** t)
    v_hat = v_new / (1.0 - beta2 ** t)
    w_new = w - lr * m_hat / (jnp.sqrt(v_hat) + eps)
    return m_new, v_new, w_new


def solution(mesh):
    p = mesh.shape["outer"] * mesh.shape["inner"]

    def body(g_emb, g_qkv, g_o, g_w1, g_w2, g_bqkv, g_b1, g_dvec, m, v, w, lr, beta1, beta2, eps, step):
        grads = (g_emb, g_qkv, g_o, g_w1, g_w2, g_bqkv, g_b1, g_dvec)
        shapes = tuple(x.shape[1:] for x in grads)
        plan = Plan(shapes, p)
        n = len(plan.big)
        stored = [as_stored(x, nj) for x, (_, nj, _) in zip(grads, plan.big)]
        small = jnp.concatenate([x.reshape(2, -1, LANES).transpose(1, 0, 2) for x in grads[n:]], axis=0)
        small = jnp.pad(small, ((0, plan.small_rows // 2 - small.shape[0]), (0, 0), (0, 0)))
        stored.append(small.reshape(-1, LANES))
        total = reduce_scatter(plan, stored).reshape(-1)
        r = lax.axis_index(AXES)
        offset = r * plan.shard - plan.start(r) * LANES
        g = lax.dynamic_slice(total, (offset,), (plan.shard,)) / p
        m_new, v_new, w_new = adam_update(g, m, v, w, lr, beta1, beta2, eps, step)
        front = max(i * plan.shard - plan.starts[i] * LANES for i in range(p))
        back = plan.window * LANES - plan.shard
        win = lax.dynamic_slice(jnp.pad(w_new, (front, back)), (front - offset,), (plan.window * LANES,))
        wb = all_gather(plan, win.reshape(plan.window, LANES))
        return (m_new, v_new, w_new) + restore(plan, wb, shapes)

    g3 = P(AXES, None, None)
    g4 = P(AXES, None, None, None)
    flat = P(AXES)
    rep = P()
    in_specs = (g3, g4, g4, g4, g4, g3, g3, g4, flat, flat, flat, rep, rep, rep, rep, rep)
    out_specs = (flat, flat, flat, rep, rep, rep, rep, rep, rep, rep, rep)
    return jax.shard_map(body, mesh=mesh, in_specs=in_specs, out_specs=out_specs, check_vma=False)
```

time: 1230 us -> 383 us (0.31)
  waiting for transfers between devices: 932 us -> 0 us
  Pallas kernels: 0 us -> 365 us
  local copies, waits for them, and re-layouts: 259 us -> 4.66 us
  between operations: 17.5 us -> 4.14 us
    unnamed x4 -> x0, waiting for transfers between devices: 932 us -> none
    pallas_call x0 -> x3, Pallas kernels: none -> 365 us  [the longest x1 235 us: reduce_scatter(): pl.pallas_call(functools.partial(rs_kernel, plan), out_shape=(pltpu.VMEM(...]
    unnamed x41 -> x7, local copies, waits for them, and re-layouts: 113 us -> 1.18 us
    reshape x12 -> x2, local copies, waits for them, and re-layouts: 104 us -> 2.22 us  [the longest x1 1.48 us: body(): wb = all_gather(plan, win.reshape(plan.window, LANES))]
    slice x11 -> x5, local copies, waits for them, and re-layouts: 40.5 us -> 1.24 us  [restore(): result.append(small[row // 2:row // 2 + nj].transpose(1, 0, 2).reshape(s))]
  transfers between devices with their start and end apart: 2 -> 0, of which waited for: 2 -> 0; matrix products, arithmetic and copies ran while one was open for 0% -> 0% of each run, Pallas kernels for 0% -> 0%
where the time goes in v3:
time: 383 us
  Pallas kernels  365 us (95%)
  other arithmetic  9.01 us (2%)
  local copies, waits for them, and re-layouts  4.66 us (1%)
  between operations  4.14 us (1%)
    pallas_call x1, Pallas kernels, reduce_scatter(): pl.pallas_call(functools.partial(rs_kernel, plan), out_shape=(pltpu.VMEM(...  235 us
    pallas_call x1, Pallas kernels, all_gather(): pl.pallas_call(functools.partial(ag_kernel, plan), out_shape=[pltpu.VMEM(...  119 us
    pallas_call x1, Pallas kernels, restore(): pl.pallas_call(functools.partial(restore_kernel, plan), out_shape=[jax.Sh...  11.6 us

profile of v3, /device:TPU:0, one launch (start us, length us, event | category | flops | bytes accessed | tf_op | source)
XLA Modules:
  0.0 383.2 jit_solution(2919000025576440504)
XLA Ops:
  4.1 0.7 reshape.123
  4.8 1.5 select_maximum_fusion
  6.3 0.0 copy-start.1
  6.3 0.0 copy-start.2
  6.3 234.8 %reduce_scatter.1 = (f32[8640,128]{1,0:T(8,128)S(1)}, f32[48,720,128]{2,1,0:T(8,128)}) custom-call(f32[24576,128]{1,0:T(8,128)} %bitcast.82, f32[27648,128]{1,0:T(8,128)} %bitcast.81, f32[9216,128]{1,0:T(8,128)} %bitcast.83, f32[36864,128]{1,0:T(8,128)} %bitcast.79, f32[36864,128]{1,0:T(8,128)} %bitcast.80, f32[336,128]{1,0:T(8,128)} %bitcast.84), custom_call_target="tpu_custom_call" | custom-call | tf_op jit(solution)/shard_map/reduce_scatter/pallas_call | solution.py:371
  241.1 0.0 copy-done.1
  241.2 0.0 copy-done.2
  241.2 7.5 %divide_subtract_fusion = (f32[1082592]{0:T(1024)S(1)}, f32[1082592]{0:T(1024)}, f32[1082592]{0:T(1024)}) fusion(f32[1082592]{0:T(1024)S(1)} %copy-done.1, f32[]{:T(128)S(6)} %copy.43, f32[]{:T(128)S(6)} %sub.25, f32[]{:T(128)S(6)} %sub.24, f32[]{:T(128)S(6)} %copy.40, f32[1105920]{0:T(1024)S(1)} %bitcast.78, s32[]{:T(128)S(6)} %select_n.67, f32[]{:T(128)S(6)} %sub.23, ...), kind=kLoop, calls=%fused_computation.2 | loop fusion | flops 15156288 | bytes 30312612 | tf_op jit(solution)/shard_map/sub | solution.py:568
  248.7 0.0 copy-start
  248.7 1.5 fusion.values
  250.2 0.6 copy-done
  250.7 118.9 %all_gather.1 = (bf16[46080,128]{1,0:T(8,128)(2,1)S(1)}, bf16[46080,128]{1,0:T(8,128)(2,1)S(1)}, bf16[46080,128]{1,0:T(8,128)(2,1)S(1)}) custom-call(f32[8640,128]{1,0:T(8,128)S(1)} %fusion.values), custom_call_target="tpu_custom_call" | custom-call | tf_op jit(solution)/shard_map/all_gather/pallas_call | solution.py:504
  369.6 11.6 %restore.1 = (bf16[24576,128]{1,0:T(8,128)(2,1)}, bf16[27648,128]{1,0:T(8,128)(2,1)}, bf16[9216,128]{1,0:T(8,128)(2,1)}, bf16[36864,128]{1,0:T(8,128)(2,1)}, bf1...) custom-call(bf16[46080,128]{1,0:T(8,128)(2,1)S(1)} %get-tuple-element.22.refs_0_, ...), custom_call_target="tpu_custom_call" | custom-call | tf_op jit(solution)/shard_map/restore/pallas_call | solution.py:545
  381.3 0.6 copy.39
  381.9 0.6 slice.20
  382.5 0.6 slice.22
  (4 shorter events, 0.0 us)
Async XLA Ops:
  6.3 234.8 %copy-start.1 = (f32[1082592]{0:T(1024)S(1)}, f32[1082592]{0:T(1024)}, u32[]{:S(2)}) copy-start(f32[1082592]{0:T(1024)} %param.26) | copy-start | bytes 12991108
  6.3 234.9 %copy-start.2 = (f32[1082592]{0:T(1024)S(1)}, f32[1082592]{0:T(1024)}, u32[]{:S(2)}) copy-start(f32[1082592]{0:T(1024)} %param.25) | copy-start | bytes 12991108
  248.7 2.1 copy-start

commit v4 on v3

--- a/solution.py
+++ b/solution.py
@@ -13,9 +13,9 @@
 ANY = pl.BlockSpec(memory_space=pl.ANY)
 LANES = 128
 TILE = 16
-SPLIT = 4
-DEEP = 4
-LEAD = 12
+SPLIT = 2
+DEEP = 2
+LEAD = 6
 BF = jnp.bfloat16
 F32 = jnp.float32
 
@@ -83,11 +83,15 @@
         return out
 
     def pairs(self):
-        out, row = [], 0
+        flat, row, kept = [], 0, 0
         for n in self.sizes[len(self.big):]:
-            out.append((row, n // (2 * LANES)))
+            flat.append((row, n // (2 * LANES)))
             row += n // LANES
-        return out
+        out = []
+        for at, nj in flat[1:] + flat[:1]:
+            out.append((at, kept, nj))
+            kept += 2 * nj
+        return out[-1:] + out[:-1]
 
 
 def as_stored(x, nj):
@@ -118,8 +122,7 @@
         return (b[0] * 2 + b[1], b[2] * 2 + self.core)
 
     def part(self, i):
-        a, s, k = lax.div(i, 3 * SPLIT), lax.rem(lax.div(i, 3), SPLIT), lax.rem(i, 3)
-        return a, k, s, a * (3 * SPLIT) + k * SPLIT + s
+        return lax.div(i, 3 * SPLIT), lax.rem(i, 3), lax.rem(i, 3 * SPLIT)
 
     def block(self, a, k, core):
         e = [1 - lax.div(a, 4), 1 - lax.rem(lax.div(a, 2), 2), 1 - lax.rem(a, 2)]
@@ -159,10 +162,12 @@
 
 
 def rs_kernel(plan, *refs):
-    n_in = len(plan.big) + 1
-    xs, flat, late_ref = refs[:n_in], refs[n_in], refs[n_in + 1]
-    early, r1, r2, r3, own, oth = refs[n_in + 2:n_in + 8]
-    own_sem, oth_sem, d_send, d_recv, s1_send, s1_recv, s2_send, s2_recv, s3_send, s3_recv = refs[n_in + 8:]
+    n_big = len(plan.big)
+    n_in = n_big + len(plan.pairs())
+    flat, late_ref = refs[n_in:n_in + 2]
+    early, r1, r2, r3, own, oth, small, odd = refs[n_in + 2:n_in + 10]
+    own_sem, oth_sem, d_send, d_recv, s1_send, s1_recv, s2_send, s2_recv, s3_send, s3_recv, tiny_sem = refs[n_in + 10:]
+    xs = refs[:n_big] + (small,)
     part = plan.part
     wave = 3 * SPLIT
     early_n = 4 * wave
@@ -171,8 +176,8 @@
     crossing = plan.crossing()
 
     def pick(i, core, issue):
-        a, k, s, _ = place.part(i)
-        row = plan.start(place.block(a, k, core)) + k * plan.unit + s * part
+        a, k, at = place.part(i)
+        row = plan.start(place.block(a, k, core)) + at * part
         for t, (lo, hi) in enumerate(plan.spans()):
 
             @pl.when((row >= lo) & (row <= hi - part))
@@ -187,7 +192,7 @@
                     issue(xs[t].at[pl.ds(at, size)], to, size)
 
     def swap(i):
-        slot = place.part(i)[3]
+        slot = i
 
         def issue(src, at, size):
             remote(src, early.at[slot, pl.ds(at, size)], d_send.at[slot], d_recv.at[slot], partner).start()
@@ -195,7 +200,7 @@
         pick(i, 1 - place.core, issue)
 
     def swap_late(i):
-        slot = place.part(i)[3]
+        slot = i
 
         def issue(src, at, size):
             remote(
@@ -225,7 +230,7 @@
 
     def fetch(i):
         to = lax.rem(i, DEEP)
-        return pltpu.make_async_copy(late_ref.at[place.part(i)[3]], oth.at[to], oth_sem.at[to])
+        return pltpu.make_async_copy(late_ref.at[i], oth.at[to], oth_sem.at[to])
 
     def hop(stage, k, slot):
         src, dst, send, recv, base = (
@@ -256,12 +261,24 @@
         lax.fori_loop(0, count, body, 0)
 
     arrive(place)
+    copies = []
+    for m, (x, (_, kept, nj)) in enumerate(zip(refs[n_big:n_in], plan.pairs())):
+        dst = odd if m == 0 else small.at[pl.ds(kept, 2 * nj)]
+        copies.append(pltpu.make_async_copy(x, dst, tiny_sem.at[m]))
+        copies[-1].start()
+    end = plan.small_size // LANES
+    small[end:, :] = jnp.zeros((plan.small_rows - end, LANES), F32)
+    for c in copies:
+        c.wait()
+    _, kept, nj = plan.pairs()[0]
+    for j in range(nj):
+        small[kept + 2 * j:kept + 2 * j + 2, :] = odd[:, j * LANES:(j + 1) * LANES]
     loop(DEEP, load)
     meet()
     loop(LEAD, swap)
 
     def first(i):
-        _, k, _, slot = place.part(i)
+        k, slot = lax.rem(i, 3), i
 
         @pl.when(i + LEAD < early_n)
         def _():
@@ -280,13 +297,13 @@
     loop(early_n, first)
 
     def prefetch(i):
-        swapped_late(place.part(i)[3]).wait_recv()
+        swapped_late(i).wait_recv()
         fetch(i).start()
 
     loop(DEEP, prefetch)
 
     def second(i):
-        _, k, _, slot = place.part(i)
+        k, slot = lax.rem(i, 3), i
 
         @pl.when(i + LEAD < early_n)
         def _():
@@ -310,7 +327,7 @@
     loop(early_n, second)
 
     def third(i):
-        _, k, _, slot = place.part(i)
+        k, slot = lax.rem(i, 3), i
         hop(1, k, slot).wait_recv()
         add(r1.at[2 * wave + slot], r2.at[slot])
 
@@ -321,7 +338,7 @@
     loop(2 * wave, third)
 
     def fourth(i):
-        _, k, _, slot = place.part(i)
+        k, slot = lax.rem(i, 3), i
         hop(2, k, slot).wait_recv()
         add(r1.at[3 * wave + slot], r3.at[slot])
 
@@ -341,13 +358,12 @@
     @pl.when(me == plan.p - 1)
     def _():
         base = plan.small_row - plan.starts[plan.p - 1]
-        for row, nj in plan.pairs():
+        for row, kept, nj in plan.pairs():
             for layer in range(2):
-                at = base + row + layer * nj
-                flat[pl.ds(at, nj), :] = stored[pl.ds(base + row + layer, nj, stride=2), :]
+                flat[pl.ds(base + row + layer * nj, nj), :] = stored[pl.ds(base + kept + layer, nj, stride=2), :]
 
     def sent(i):
-        _, k, _, slot = place.part(i)
+        k, slot = lax.rem(i, 3), i
         swapped(slot).wait_send()
         swapped_late(slot).wait_send()
         hop(0, k, slot).wait_send()
@@ -377,8 +393,10 @@
         in_specs=[ANY] * len(xs),
         out_specs=(pl.BlockSpec(memory_space=pltpu.VMEM), ANY),
         scratch_shapes=[pltpu.VMEM((n, plan.part, LANES), F32) for n in slots]
+        + [pltpu.VMEM((plan.small_rows, LANES), F32), pltpu.VMEM(xs[len(plan.big)].shape, F32)]
         + [dma((DEEP,)), dma((DEEP,))]
-        + [dma((n * wave,)) for n in (8, 8, 4, 4, 2, 2, 1, 1)],
+        + [dma((n * wave,)) for n in (8, 8, 4, 4, 2, 2, 1, 1)]
+        + [dma((len(plan.pairs()),))],
         compiler_params=pltpu.CompilerParams(
             collective_id=0, has_side_effects=True, vmem_limit_bytes=used << 20
         ),
@@ -411,9 +429,9 @@
     def _():
         base = plan.small_row - plan.starts[plan.p - 1]
         tiny[...] = jnp.zeros_like(tiny)
-        for row, nj in plan.pairs():
+        for row, kept, nj in plan.pairs():
             for layer in range(2):
-                tiny[pl.ds(row + layer, nj, stride=2), :] = values[pl.ds(base + row + layer * nj, nj), :]
+                tiny[pl.ds(kept + layer, nj, stride=2), :] = values[pl.ds(base + row + layer * nj, nj), :]
         win[pl.ds(base, tiny.shape[0]), :] = tiny[...].astype(BF)
 
     def rows_of(k, e, s, core):
@@ -426,7 +444,7 @@
         return (slot[e] * 3 + k) * SPLIT + s
 
     def src(k, e, s):
-        return win.at[pl.ds(k * plan.unit + s * part, part)] if e == here else rows_of(k, e, s, place.core)
+        return win.at[pl.ds((3 * s + k) * part, part)] if e == here else rows_of(k, e, s, place.core)
 
     sent = []
 
@@ -463,14 +481,16 @@
         for k in range(3):
             share(k, here, s)
     rows = 3 * TILE
-    for k in range(3):
-
-        def keep(i, _, k=k):
-            at = pl.multiple_of(i * rows, rows)
-            w_refs[k][pl.ds(pl.multiple_of(me * unit + at, TILE), rows), :] = win[pl.ds(k * unit + at, rows), :]
-            return 0
-
-        lax.fori_loop(0, unit // rows, keep, 0)
+    for s in range(SPLIT):
+        for k in range(3):
+
+            def keep(i, _, k=k, s=s):
+                at = pl.multiple_of(i * rows, rows)
+                to = pl.ds(pl.multiple_of(me * unit + s * part + at, TILE), rows)
+                w_refs[k][to, :] = win[pl.ds((3 * s + k) * part + at, rows), :]
+                return 0
+
+            lax.fori_loop(0, part // rows, keep, 0)
     for e in list(slot)[1:]:
         for s in range(SPLIT):
             for k in range(3):
@@ -492,8 +512,8 @@
         row, lane = lax.broadcasted_iota(jnp.int32, shape, 0), lax.broadcasted_iota(jnp.int32, shape, 1)
         at = (lax.rem(row, 8) * nj + lax.div(row, 8)) * LANES + lane
         cut = r * plan.shard - plan.starts[r] * LANES
-        gap = plan.starts[r] - plan.starts[r - 1] - 2 * unit
-        before = w_refs[2][pl.ds((r - 1) * unit + gap, size), :]
+        gap = plan.starts[r] - plan.starts[r - 1] - plan.window
+        before = w_refs[2][pl.ds(r * unit + gap, size), :]
         rows = pl.ds(r * unit, size)
         w_refs[0][rows, :] = jnp.where(at < cut, before.astype(F32), w_refs[0][rows, :].astype(F32)).astype(BF)
 
@@ -519,20 +539,25 @@
 
 def restore_kernel(plan, *refs):
     w_refs, outs, out_sem = refs[:3], refs[3:-1], refs[-1]
-    p = plan.p
-    spans = plan.spans()[:-1] + [(plan.small_row, plan.small_row + small_rows(plan))]
+    p, part = plan.p, plan.part
     copies = []
+
+    def copy(r, x, y, dst):
+        for n in range(x // part, -(-y // part)):
+            lo, hi = max(x, n * part), min(y, (n + 1) * part)
+            src = w_refs[n % 3].at[pl.ds(r * plan.unit + n // 3 * part + lo - n * part, hi - lo)]
+            copies.append(pltpu.make_async_copy(src, dst(lo - x, hi - lo), out_sem.at[len(copies)]))
+
     for r in range(p):
         lo = plan.starts[r]
-        hi = plan.starts[r + 1] if r + 1 < p else spans[-1][1]
-        for k in range(3):
-            first = lo + k * plan.unit
-            for t, (x, y) in enumerate(spans):
-                x, y = max(x, first), min(y, hi, first + plan.unit)
-                if x < y:
-                    src = w_refs[k].at[pl.ds(r * plan.unit + x - first, y - x)]
-                    dst = outs[t].at[pl.ds(x - spans[t][0], y - x)]
-                    copies.append(pltpu.make_async_copy(src, dst, out_sem.at[len(copies)]))
+        hi = plan.starts[r + 1] if r + 1 < p else plan.small_row
+        for t, (a, b) in enumerate(plan.spans()[:-1]):
+            x, y = max(a, lo), min(b, hi)
+            if x < y:
+                copy(r, x - lo, y - lo, lambda at, size, t=t, x=x, a=a: outs[t].at[pl.ds(x - a + at, size)])
+    base = plan.small_row - plan.starts[p - 1]
+    for out, (_, kept, nj) in zip(outs[len(plan.big):], plan.pairs()):
+        copy(p - 1, base + kept, base + kept + out.shape[0], lambda at, size, out=out: out.at[pl.ds(at, size)])
     for c in copies:
         c.start()
     for c in copies:
@@ -545,17 +570,17 @@
     outs = pl.pallas_call(
         functools.partial(restore_kernel, plan),
         out_shape=[jax.ShapeDtypeStruct((rows, LANES), BF) for rows, _, _ in plan.big]
-        + [jax.ShapeDtypeStruct((small_rows(plan), LANES), BF)],
+        + [jax.ShapeDtypeStruct((2 * nj if m else -(-2 * nj // TILE) * TILE, LANES), BF)
+           for m, (_, _, nj) in enumerate(plan.pairs())],
         in_specs=[ANY] * 3,
-        out_specs=[ANY] * (n + 1),
-        scratch_shapes=[dma((3 * plan.p + n + 1,))],
+        out_specs=[ANY] * len(shapes),
+        scratch_shapes=[dma((3 * SPLIT * plan.p + 3 * n,))],
         compiler_params=pltpu.CompilerParams(vmem_limit_bytes=1 << 20),
         name="restore",
     )(*gathered)
     result = [from_stored(x, nj, s) for x, (_, nj, _), s in zip(outs, plan.big, shapes)]
-    small = outs[n].reshape(-1, 2, LANES)
-    for (row, nj), s in zip(plan.pairs(), shapes[n:]):
-        result.append(small[row // 2:row // 2 + nj].transpose(1, 0, 2).reshape(s))
+    for x, (_, _, nj), s in zip(outs[n:], plan.pairs(), shapes[n:]):
+        result.append(x[:2 * nj].reshape(nj, 2, LANES).transpose(1, 0, 2).reshape(s))
     return tuple(result)
 
 
@@ -578,9 +603,8 @@
         plan = Plan(shapes, p)
         n = len(plan.big)
         stored = [as_stored(x, nj) for x, (_, nj, _) in zip(grads, plan.big)]
-        small = jnp.concatenate([x.reshape(2, -1, LANES).transpose(1, 0, 2) for x in grads[n:]], axis=0)
-        small = jnp.pad(small, ((0, plan.small_rows // 2 - small.shape[0]), (0, 0), (0, 0)))
-        stored.append(small.reshape(-1, LANES))
+        stored.append(grads[n].reshape(shapes[n]))
+        stored += [x.reshape(2, -1, LANES).transpose(1, 0, 2).reshape(-1, LANES) for x in grads[n + 1:]]
         total = reduce_scatter(plan, stored).reshape(-1)
         r = lax.axis_index(AXES)
         offset = r * plan.shard - plan.start(r) * LANES

time: 383 us -> 380 us (level)
  no operation moved by 1% of the time
where the time goes in v4:
time: 380 us; the launch traced here: 379 us
  Pallas kernels  365 us (96%)
  other arithmetic  7.51 us (2%)
  between operations  4.15 us (1%)
    pallas_call x1, Pallas kernels, reduce_scatter(): pl.pallas_call(functools.partial(rs_kernel, plan), out_shape=(pltpu.VMEM(...  234 us
    pallas_call x1, Pallas kernels, all_gather(): pl.pallas_call(functools.partial(ag_kernel, plan), out_shape=[pltpu.VMEM(...  118 us
    pallas_call x1, Pallas kernels, restore(): pl.pallas_call(functools.partial(restore_kernel, plan), out_shape=[jax.Sh...  12.1 us

profile of v4, /device:TPU:0, one launch (start us, length us, event | category | flops | bytes accessed | tf_op | source)
XLA Modules:
  0.0 378.9 jit_solution(6974938274648752247)
XLA Ops:
  4.1 0.0 copy-start.1
  4.1 0.0 copy-start.2
  4.1 234.5 %reduce_scatter.1 = (f32[8640,128]{1,0:T(8,128)S(1)}, f32[24,1440,128]{2,1,0:T(8,128)}) custom-call(f32[24576,128]{1,0:T(8,128)} %bitcast.85, f32[27648,128]{1,0:T(8,128)} %bitcast.84, f32[9216,128]{1,0:T(8,128)} %bitcast.86, f32[36864,128]{1,0:T(8,128)} %bitcast.82, f32[36864,128]{1,0:T(8,128)} %bitcast.83, f32[2,2304]{1,0:T(2,128)} %bitcast.90, ...), custom_call_target="tpu_custom_call" | custom-call | tf_op jit(solution)/shard_map/reduce_scatter/pallas_call | solution.py:387
  238.6 0.0 copy-done.1
  238.6 0.0 copy-done.2
  238.6 7.5 %divide_subtract_fusion = (f32[1082592]{0:T(1024)S(1)}, f32[1082592]{0:T(1024)}, f32[1082592]{0:T(1024)}) fusion(f32[1082592]{0:T(1024)S(1)} %copy-done.1, f32[]{:T(128)S(6)} %copy.41, f32[]{:T(128)S(6)} %sub.25, f32[]{:T(128)S(6)} %sub.24, f32[]{:T(128)S(6)} %copy.38, f32[1105920]{0:T(1024)S(1)} %bitcast.81, s32[]{:T(128)S(6)} %select_n.67, f32[]{:T(128)S(6)} %sub.23, ...), kind=kLoop, calls=%fused_computation.2 | loop fusion | flops 15156288 | bytes 30312612 | tf_op jit(solution)/shard_map/sub | solution.py:593
  246.1 0.0 copy-start
  246.1 1.5 fusion.values
  247.6 0.6 copy-done
  248.2 118.0 %all_gather.1 = (bf16[46080,128]{1,0:T(8,128)(2,1)S(1)}, bf16[46080,128]{1,0:T(8,128)(2,1)S(1)}, bf16[46080,128]{1,0:T(8,128)(2,1)S(1)}) custom-call(f32[8640,128]{1,0:T(8,128)S(1)} %fusion.values), custom_call_target="tpu_custom_call" | custom-call | tf_op jit(solution)/shard_map/all_gather/pallas_call | solution.py:524
  366.1 12.1 %restore.1 = (bf16[24576,128]{1,0:T(8,128)(2,1)}, bf16[27648,128]{1,0:T(8,128)(2,1)}, bf16[9216,128]{1,0:T(8,128)(2,1)}, bf16[36864,128]{1,0:T(8,128)(2,1)}, bf1...) custom-call(bf16[46080,128]{1,0:T(8,128)(2,1)S(1)} %get-tuple-element., ...), custom_call_target="tpu_custom_call" | custom-call | tf_op jit(solution)/shard_map/restore/pallas_call | solution.py:570
  378.3 0.6 copy.37
  (3 shorter events, 0.0 us)
Async XLA Ops:
  4.1 234.5 %copy-start.1 = (f32[1082592]{0:T(1024)S(1)}, f32[1082592]{0:T(1024)}, u32[]{:S(2)}) copy-start(f32[1082592]{0:T(1024)} %param.26) | copy-start | bytes 12991108
  4.1 234.5 %copy-start.2 = (f32[1082592]{0:T(1024)S(1)}, f32[1082592]{0:T(1024)}, u32[]{:S(2)}) copy-start(f32[1082592]{0:T(1024)} %param.25) | copy-start | bytes 12991108
  246.1 2.1 copy-start

commit v5 on v4

--- a/solution.py
+++ b/solution.py
@@ -13,9 +13,10 @@
 ANY = pl.BlockSpec(memory_space=pl.ANY)
 LANES = 128
 TILE = 16
-SPLIT = 2
-DEEP = 2
-LEAD = 6
+SPLIT = 4
+HALVES = 2
+DEEP = 4
+LEAD = 12
 BF = jnp.bfloat16
 F32 = jnp.float32
 
@@ -42,6 +43,7 @@
         self.part = -(-need // (3 * SPLIT * TILE)) * TILE
         self.unit = SPLIT * self.part
         self.window = 3 * self.unit
+        self.piece = self.unit // HALVES
         self.small_rows = self.starts[p - 1] + self.window - self.small_row
 
     def group(self, row):
@@ -81,6 +83,20 @@
             hi = jnp.minimum(first + self.window, flat + n)
             out.append((nj, lo - first, lax.div(jnp.maximum(hi - lo, 0), 8 * nj)))
         return out
+
+    def sort(self, first, lo, hi, spill, move):
+        for nj, row, groups in self.segments(first):
+            size = 8 * nj
+            more = size - 1 if spill else 0
+            done, todo = [
+                jnp.minimum(groups, lax.div(jnp.maximum(x - row, 0) + more, size)) if x else 0 for x in (lo, hi)
+            ]
+
+            def body(i, _, nj=nj, row=row, done=done, size=size):
+                move(nj, pl.multiple_of(row + (done + i) * size, TILE))
+                return 0
+
+            lax.fori_loop(0, todo - done, body, 0)
 
     def pairs(self):
         flat, row, kept = [], 0, 0
@@ -337,23 +353,23 @@
 
     loop(2 * wave, third)
 
-    def fourth(i):
-        k, slot = lax.rem(i, 3), i
-        hop(2, k, slot).wait_recv()
-        add(r1.at[3 * wave + slot], r3.at[slot])
-
-    loop(wave, fourth)
-
     me = place.owner(dims_of(0), (0, 0, 0), place.core)
+    first_row = plan.start(me)
     stored = r1.at[pl.ds(3 * wave, wave)].reshape(plan.window, LANES)
-    for nj, row, groups in plan.segments(plan.start(me)):
-
-        def sort(i, nj=nj, row=row):
-            base = pl.multiple_of(row + i * 8 * nj, TILE)
-            for j in range(nj):
-                flat[pl.ds(base + j, 8, stride=nj), :] = stored[pl.ds(base + j * 8, 8), :]
-
-        loop(groups, sort)
+
+    def move(nj, base):
+        for j in range(nj):
+            flat[pl.ds(base + j, 8, stride=nj), :] = stored[pl.ds(base + j * 8, 8), :]
+
+    for s in range(SPLIT):
+
+        def fourth(j, s=s):
+            slot = 3 * s + j
+            hop(2, j, slot).wait_recv()
+            add(r1.at[3 * wave + slot], r3.at[slot])
+
+        loop(3, fourth)
+        plan.sort(first_row, 3 * s * part, 3 * (s + 1) * part, False, move)
 
     @pl.when(me == plan.p - 1)
     def _():
@@ -407,23 +423,19 @@
 
 def ag_kernel(plan, values, *refs):
     w_refs, (win, tiny, s_send, s_recv, d_send, d_recv) = refs[:3], refs[3:]
-    part, unit = plan.part, plan.unit
+    part, unit = plan.piece, plan.unit
     place = Place()
     partner = place.partner()
     here = (0, 0, 0)
     me = place.owner(dims_of(0), here, place.core)
     arrive(place)
 
-    for nj, row, groups in plan.segments(plan.start(me)):
-
-        def sort(i, _, nj=nj, row=row):
-            base = pl.multiple_of(row + i * 8 * nj, TILE)
-            for j in range(0, nj, 2):
-                pair = [values[pl.ds(base + j + h, 8, stride=nj), :] for h in range(2)]
-                win[pl.ds(base + j * 8, TILE), :] = jnp.concatenate(pair, axis=0).astype(BF)
-            return 0
-
-        lax.fori_loop(0, groups, sort, 0)
+    first_row = plan.start(me)
+
+    def move(nj, base):
+        for j in range(0, nj, 2):
+            pair = [values[pl.ds(base + j + h, 8, stride=nj), :] for h in range(2)]
+            win[pl.ds(base + j * 8, TILE), :] = jnp.concatenate(pair, axis=0).astype(BF)
 
     @pl.when(me == plan.p - 1)
     def _():
@@ -441,7 +453,7 @@
     slot = {here: 0, (1, 0, 0): 1, (0, 1, 0): 2, (0, 0, 1): 3, (1, 1, 0): 4, (1, 0, 1): 5, (0, 1, 1): 6, (1, 1, 1): 7}
 
     def index(k, e, s):
-        return (slot[e] * 3 + k) * SPLIT + s
+        return (slot[e] * 3 + k) * HALVES + s
 
     def src(k, e, s):
         return win.at[pl.ds((3 * s + k) * part, part)] if e == here else rows_of(k, e, s, place.core)
@@ -472,16 +484,18 @@
         i, dst = index(k, e, s), rows_of(k, e, s, 1 - place.core)
         return remote(dst, dst, d_send.at[i], d_recv.at[i], partner)
 
-    meet()
-    for n in range(3):
-        for s in range(SPLIT):
+    for s in range(HALVES):
+        plan.sort(first_row, 3 * s * part, 3 * (s + 1) * part, True, move)
+        if s == 0:
+            meet()
+        for n in range(3):
             for k in range(3):
                 send(k, here, s, n)
-    for s in range(SPLIT):
+    for s in range(HALVES):
         for k in range(3):
             share(k, here, s)
     rows = 3 * TILE
-    for s in range(SPLIT):
+    for s in range(HALVES):
         for k in range(3):
 
             def keep(i, _, k=k, s=s):
@@ -492,7 +506,7 @@
 
             lax.fori_loop(0, part // rows, keep, 0)
     for e in list(slot)[1:]:
-        for s in range(SPLIT):
+        for s in range(HALVES):
             for k in range(3):
                 arrival(k, e, s).wait_recv()
                 for n in range(1, 3):
@@ -500,7 +514,7 @@
                         send(k, e, s, n)
                 share(k, e, s)
     for e in slot:
-        for s in range(SPLIT):
+        for s in range(HALVES):
             for k in range(3):
                 shared(k, e, s).wait_recv()
     for copy in sent:
@@ -520,7 +534,7 @@
 
 def all_gather(plan, win):
     dma = pltpu.SemaphoreType.DMA
-    n = 8 * 3 * SPLIT
+    n = 8 * 3 * HALVES
     return pl.pallas_call(
         functools.partial(ag_kernel, plan),
         out_shape=[pltpu.VMEM((plan.p * plan.unit, LANES), BF)] * 3,
@@ -539,7 +553,7 @@
 
 def restore_kernel(plan, *refs):
     w_refs, outs, out_sem = refs[:3], refs[3:-1], refs[-1]
-    p, part = plan.p, plan.part
+    p, part = plan.p, plan.piece
     copies = []
 
     def copy(r, x, y, dst):
@@ -574,7 +588,7 @@
            for m, (_, _, nj) in enumerate(plan.pairs())],
         in_specs=[ANY] * 3,
         out_specs=[ANY] * len(shapes),
-        scratch_shapes=[dma((3 * SPLIT * plan.p + 3 * n,))],
+        scratch_shapes=[dma((3 * HALVES * plan.p + 3 * n,))],
         compiler_params=pltpu.CompilerParams(vmem_limit_bytes=1 << 20),
         name="restore",
     )(*gathered)
@@ -588,8 +602,8 @@
     t = step.astype(jnp.float32)
     m_new = beta1 * m + (1.0 - beta1) * g
     v_new = beta2 * v + (1.0 - beta2) * (g * g)
-    m_hat = m_new / (1.0 - beta1 ** t)
-    v_hat = v_new / (1.0 - beta2 ** t)
+    m_hat = m_new * (1.0 / (1.0 - beta1 ** t))
+    v_hat = v_new * (1.0 / (1.0 - beta2 ** t))
     w_new = w - lr * m_hat / (jnp.sqrt(v_hat) + eps)
     return m_new, v_new, w_new
 

time: 380 us -> 378 us (level)
  no operation moved by 1% of the time
where the time goes in v5:
time: 378 us
  Pallas kernels  364 us (96%)
  other arithmetic  7.58 us (2%)
  between operations  4.23 us (1%)
    pallas_call x1, Pallas kernels, reduce_scatter(): pl.pallas_call(functools.partial(rs_kernel, plan), out_shape=(pltpu.VMEM(...  234 us
    pallas_call x1, Pallas kernels, all_gather(): pl.pallas_call(functools.partial(ag_kernel, plan), out_shape=[pltpu.VMEM(...  118 us
    pallas_call x1, Pallas kernels, restore(): pl.pallas_call(functools.partial(restore_kernel, plan), out_shape=[jax.Sh...  12.1 us
    sub x1, other arithmetic, adam_update(): w_new = w - lr * m_hat / (jnp.sqrt(v_hat) + eps)  7.58 us

profile of v5, /device:TPU:0, one launch (start us, length us, event | category | flops | bytes accessed | tf_op | source)
XLA Modules:
  0.0 378.2 jit_solution(17470944680756529066)
XLA Ops:
  4.1 0.0 copy-start.1
  4.2 0.0 copy-start.2
  4.2 233.6 %reduce_scatter.1 = (f32[8640,128]{1,0:T(8,128)S(1)}, f32[48,720,128]{2,1,0:T(8,128)}) custom-call(f32[24576,128]{1,0:T(8,128)} %bitcast.85, f32[27648,128]{1,0:T(8,128)} %bitcast.84, f32[9216,128]{1,0:T(8,128)} %bitcast.86, f32[36864,128]{1,0:T(8,128)} %bitcast.82, f32[36864,128]{1,0:T(8,128)} %bitcast.83, f32[2,2304]{1,0:T(2,128)} %bitcast.90, ...), custom_call_target="tpu_custom_call" | custom-call | tf_op jit(solution)/shard_map/reduce_scatter/pallas_call | solution.py:403
  237.8 0.0 copy-done.1
  237.8 0.0 copy-done.2
  237.8 7.6 %divide_subtract_fusion = (f32[1082592]{0:T(1024)S(1)}, f32[1082592]{0:T(1024)}, f32[1082592]{0:T(1024)}) fusion(f32[1082592]{0:T(1024)S(1)} %copy-done.1, f32[]{:T(128)S(6)} %copy.41, f32[]{:T(128)S(6)} %div.18, f32[]{:T(128)S(6)} %div.17, f32[]{:T(128)S(6)} %copy.38, f32[1105920]{0:T(1024)S(1)} %bitcast.81, s32[]{:T(128)S(6)} %select_n.67, f32[]{:T(128)S(6)} %sub.23, ...), kind=kLoop, calls=%fused_computation.2 | loop fusion | flops 15156288 | bytes 30312612 | tf_op jit(solution)/shard_map/sub | solution.py:607
  245.4 0.0 copy-start
  245.4 1.5 fusion.values
  246.9 0.6 copy-done
  247.5 118.0 %all_gather.1 = (bf16[46080,128]{1,0:T(8,128)(2,1)S(1)}, bf16[46080,128]{1,0:T(8,128)(2,1)S(1)}, bf16[46080,128]{1,0:T(8,128)(2,1)S(1)}) custom-call(f32[8640,128]{1,0:T(8,128)S(1)} %fusion.values), custom_call_target="tpu_custom_call" | custom-call | tf_op jit(solution)/shard_map/all_gather/pallas_call | solution.py:538
  365.4 12.1 %restore.1 = (bf16[24576,128]{1,0:T(8,128)(2,1)}, bf16[27648,128]{1,0:T(8,128)(2,1)}, bf16[9216,128]{1,0:T(8,128)(2,1)}, bf16[36864,128]{1,0:T(8,128)(2,1)}, bf1...) custom-call(bf16[46080,128]{1,0:T(8,128)(2,1)S(1)} %get-tuple-element., ...), custom_call_target="tpu_custom_call" | custom-call | tf_op jit(solution)/shard_map/restore/pallas_call | solution.py:584
  377.6 0.6 copy.37
  (3 shorter events, 0.0 us)
Async XLA Ops:
  4.1 233.7 %copy-start.1 = (f32[1082592]{0:T(1024)S(1)}, f32[1082592]{0:T(1024)}, u32[]{:S(2)}) copy-start(f32[1082592]{0:T(1024)} %param.26) | copy-start | bytes 12991108
  4.2 233.7 %copy-start.2 = (f32[1082592]{0:T(1024)S(1)}, f32[1082592]{0:T(1024)}, u32[]{:S(2)}) copy-start(f32[1082592]{0:T(1024)} %param.25) | copy-start | bytes 12991108
  245.4 2.1 copy-start

commit v6 on v5

--- a/solution.py
+++ b/solution.py
@@ -15,7 +15,9 @@
 TILE = 16
 SPLIT = 4
 HALVES = 2
-DEEP = 4
+DEEP = 2
+PAD = 128
+BLOCK = 133
 LEAD = 12
 BF = jnp.bfloat16
 F32 = jnp.float32
@@ -84,6 +86,10 @@
             out.append((nj, lo - first, lax.div(jnp.maximum(hi - lo, 0), 8 * nj)))
         return out
 
+    def shift(self, r, first):
+        offset = r * self.shard - first * LANES
+        return lax.div(offset, LANES), lax.rem(offset, LANES)
+
     def sort(self, first, lo, hi, spill, move):
         for nj, row, groups in self.segments(first):
             size = 8 * nj
@@ -181,8 +187,11 @@
     n_big = len(plan.big)
     n_in = n_big + len(plan.pairs())
     flat, late_ref = refs[n_in:n_in + 2]
-    early, r1, r2, r3, own, oth, small, odd = refs[n_in + 2:n_in + 10]
-    own_sem, oth_sem, d_send, d_recv, s1_send, s1_recv, s2_send, s2_recv, s3_send, s3_recv, tiny_sem = refs[n_in + 10:]
+    early, r1, r2, own, oth, small, odd = refs[n_in + 2:n_in + 9]
+    own_sem, oth_sem, d_send, d_recv, s1_send, s1_recv, s2_send, s2_recv, s3_send, s3_recv, tiny_sem, free = refs[
+        n_in + 9:
+    ]
+    r3 = early
     xs = refs[:n_big] + (small,)
     part = plan.part
     wave = 3 * SPLIT
@@ -342,6 +351,14 @@
 
     loop(early_n, second)
 
+    def gone(i):
+        hop(0, lax.rem(i, 3), i).wait_send()
+
+    loop(wave, gone)
+    for d in range(3):
+        pl.semaphore_signal(free, inc=1, device_id=place.flipped(d), device_id_type=MESH)
+    pl.semaphore_wait(free, 3)
+
     def third(i):
         k, slot = lax.rem(i, 3), i
         hop(1, k, slot).wait_recv()
@@ -382,7 +399,10 @@
         k, slot = lax.rem(i, 3), i
         swapped(slot).wait_send()
         swapped_late(slot).wait_send()
-        hop(0, k, slot).wait_send()
+
+        @pl.when(i >= wave)
+        def _():
+            hop(0, k, slot).wait_send()
 
         @pl.when(i < 2 * wave)
         def _():
@@ -398,8 +418,8 @@
 def reduce_scatter(plan, xs):
     dma = pltpu.SemaphoreType.DMA
     wave = 3 * SPLIT
-    slots = [4 * wave, 4 * wave, 2 * wave, wave, DEEP, DEEP]
-    used = (sum(slots) * plan.part * LANES * 4 >> 20) + 2
+    slots = [4 * wave, 4 * wave, 2 * wave, DEEP, DEEP]
+    used = sum(slots) * plan.part * LANES * 4 + (5 << 19)
     g, _ = pl.pallas_call(
         functools.partial(rs_kernel, plan),
         out_shape=(
@@ -412,9 +432,9 @@
         + [pltpu.VMEM((plan.small_rows, LANES), F32), pltpu.VMEM(xs[len(plan.big)].shape, F32)]
         + [dma((DEEP,)), dma((DEEP,))]
         + [dma((n * wave,)) for n in (8, 8, 4, 4, 2, 2, 1, 1)]
-        + [dma((len(plan.pairs()),))],
+        + [dma((len(plan.pairs()),)), pltpu.SemaphoreType.REGULAR],
         compiler_params=pltpu.CompilerParams(
-            collective_id=0, has_side_effects=True, vmem_limit_bytes=used << 20
+            collective_id=0, has_side_effects=True, vmem_limit_bytes=used
         ),
         name="reduce_scatter",
     )(*xs)
@@ -431,10 +451,20 @@
     arrive(place)
 
     first_row = plan.start(me)
+    down, right = plan.shift(me, first_row)
+
+    def value(row, n, stride=1):
+        at = row - down + PAD
+        lane = lax.broadcasted_iota(jnp.int32, (n, LANES), 1)
+        if stride == 1:
+            here, before = values[pl.ds(at, n), :], values[pl.ds(at - 1, n), :]
+        else:
+            here, before = values[pl.ds(at, n, stride=stride), :], values[pl.ds(at - 1, n, stride=stride), :]
+        return jnp.where(lane >= right, here, before)
 
     def move(nj, base):
         for j in range(0, nj, 2):
-            pair = [values[pl.ds(base + j + h, 8, stride=nj), :] for h in range(2)]
+            pair = [value(base + j + h, 8, nj) for h in range(2)]
             win[pl.ds(base + j * 8, TILE), :] = jnp.concatenate(pair, axis=0).astype(BF)
 
     @pl.when(me == plan.p - 1)
@@ -443,7 +473,7 @@
         tiny[...] = jnp.zeros_like(tiny)
         for row, kept, nj in plan.pairs():
             for layer in range(2):
-                tiny[pl.ds(kept + layer, nj, stride=2), :] = values[pl.ds(base + row + layer * nj, nj), :]
+                tiny[pl.ds(kept + layer, nj, stride=2), :] = value(base + row + layer * nj, nj)
         win[pl.ds(base, tiny.shape[0]), :] = tiny[...].astype(BF)
 
     def rows_of(k, e, s, core):
@@ -542,7 +572,7 @@
         out_specs=[pl.BlockSpec(memory_space=pltpu.VMEM)] * 3,
         scratch_shapes=[pltpu.VMEM((plan.window, LANES), BF), pltpu.VMEM((small_rows(plan), LANES), F32)]
         + [dma((n,))] * 4,
-        compiler_params=pltpu.CompilerParams(collective_id=1, has_side_effects=True, vmem_limit_bytes=8 << 20),
+        compiler_params=pltpu.CompilerParams(collective_id=1, has_side_effects=True, vmem_limit_bytes=4 << 20),
         name="all_gather",
     )(win)
 
@@ -589,7 +619,7 @@
         in_specs=[ANY] * 3,
         out_specs=[ANY] * len(shapes),
         scratch_shapes=[dma((3 * HALVES * plan.p + 3 * n,))],
-        compiler_params=pltpu.CompilerParams(vmem_limit_bytes=1 << 20),
+        compiler_params=pltpu.CompilerParams(vmem_limit_bytes=4 << 20),
         name="restore",
     )(*gathered)
     result = [from_stored(x, nj, s) for x, (_, nj, _), s in zip(outs, plan.big, shapes)]
@@ -598,14 +628,51 @@
     return tuple(result)
 
 
-def adam_update(g, m, v, w, lr, beta1, beta2, eps, step):
-    t = step.astype(jnp.float32)
-    m_new = beta1 * m + (1.0 - beta1) * g
-    v_new = beta2 * v + (1.0 - beta2) * (g * g)
-    m_hat = m_new * (1.0 / (1.0 - beta1 ** t))
-    v_hat = v_new * (1.0 / (1.0 - beta2 ** t))
-    w_new = w - lr * m_hat / (jnp.sqrt(v_hat) + eps)
-    return m_new, v_new, w_new
+def update_kernel(plan, table, g, m, v, w, m_out, v_out, w_out, z):
+    step = pl.program_id(0)
+    me = lax.axis_index("outer") * 4 + lax.axis_index("inner")
+    down, right = plan.shift(me, plan.start(me))
+    lane = lax.broadcasted_iota(jnp.int32, (8, LANES), 1)
+    left = lax.rem(LANES - right, LANES)
+    beta1, gain1, beta2, gain2, scale1, scale2, lr, eps = [table[8 * n:8 * n + 8, :] for n in range(8)]
+    size = 8 * LANES
+    last = -(-plan.shard // size) - 1
+    unroll = 7
+
+    def body(i, _):
+        for t in range(unroll):
+            b = jnp.minimum(i * unroll + t, last - step * BLOCK)
+            row = (step * BLOCK + b) * 8
+            x0, x1 = g[pl.ds(row + down, 8), :], g[pl.ds(row + down + 1, 8), :]
+            grad = pltpu.roll(jnp.where(lane >= right, x0, x1), left, 1) * (1.0 / plan.p)
+            at = pl.ds(pl.multiple_of(b * size, size), size)
+            m_new = beta1 * m[at].reshape(8, LANES) + gain1 * grad
+            v_new = beta2 * v[at].reshape(8, LANES) + gain2 * (grad * grad)
+            m_hat = m_new * scale1
+            v_hat = v_new * scale2
+            w_new = w[at].reshape(8, LANES) - lr * m_hat / (jnp.sqrt(v_hat) + eps)
+            m_out[at] = m_new.reshape(size)
+            v_out[at] = v_new.reshape(size)
+            w_out[at] = w_new.reshape(size)
+            z[pl.ds(pl.multiple_of(row + PAD, 8), 8), :] = pltpu.roll(w_new, right, 1)
+        return 0
+
+    lax.fori_loop(0, BLOCK // unroll, body, 0)
+
+
+def update(plan, table, g, m, v, w):
+    flat = jax.ShapeDtypeStruct((plan.shard,), F32)
+    part = pl.BlockSpec((BLOCK * 8 * LANES,), lambda i: (i,))
+    whole = pl.BlockSpec(memory_space=pltpu.VMEM)
+    return pl.pallas_call(
+        functools.partial(update_kernel, plan),
+        grid=(pl.cdiv(plan.shard, BLOCK * 8 * LANES),),
+        out_shape=(flat, flat, flat, pltpu.VMEM((plan.window + 2 * PAD, LANES), F32)),
+        in_specs=[whole, whole, part, part, part],
+        out_specs=(part, part, part, whole),
+        compiler_params=pltpu.CompilerParams(vmem_limit_bytes=8 << 20),
+        name="update",
+    )(table, g, m, v, w)
 
 
 def solution(mesh):
@@ -619,15 +686,13 @@
         stored = [as_stored(x, nj) for x, (_, nj, _) in zip(grads, plan.big)]
         stored.append(grads[n].reshape(shapes[n]))
         stored += [x.reshape(2, -1, LANES).transpose(1, 0, 2).reshape(-1, LANES) for x in grads[n + 1:]]
-        total = reduce_scatter(plan, stored).reshape(-1)
-        r = lax.axis_index(AXES)
-        offset = r * plan.shard - plan.start(r) * LANES
-        g = lax.dynamic_slice(total, (offset,), (plan.shard,)) / p
-        m_new, v_new, w_new = adam_update(g, m, v, w, lr, beta1, beta2, eps, step)
-        front = max(i * plan.shard - plan.starts[i] * LANES for i in range(p))
-        back = plan.window * LANES - plan.shard
-        win = lax.dynamic_slice(jnp.pad(w_new, (front, back)), (front - offset,), (plan.window * LANES,))
-        wb = all_gather(plan, win.reshape(plan.window, LANES))
+        t = step.astype(F32)
+        scale1, scale2 = 1.0 / (1.0 - beta1 ** t), 1.0 / (1.0 - beta2 ** t)
+        table = jnp.stack([beta1, 1.0 - beta1, beta2, 1.0 - beta2, scale1, scale2, lr, eps])
+        table = jnp.broadcast_to(table[:, None, None], (8, 8, LANES)).reshape(64, LANES)
+        total = reduce_scatter(plan, stored)
+        m_new, v_new, w_new, values = update(plan, table, total, m, v, w)
+        wb = all_gather(plan, values)
         return (m_new, v_new, w_new) + restore(plan, wb, shapes)
 
     g3 = P(AXES, None, None)

time: 378 us -> 401 us (1.061)
  Pallas kernels: 364 us -> 392 us
  other arithmetic: 7.58 us -> 0 us
    pallas_call x0 -> x1, Pallas kernels: none -> 28 us  [update(): pl.pallas_call(functools.partial(update_kernel, plan), grid=(pl.cdiv(plan...]
    sub x1 -> x0, other arithmetic: 7.58 us -> none  [adam_update(): w_new = w - lr * m_hat / (jnp.sqrt(v_hat) + eps)]
where the time goes in v6:
time: 401 us; the launch traced here: 400 us
  Pallas kernels  392 us (98%)
  between operations  4.13 us (1%)
    pallas_call x1, Pallas kernels, reduce_scatter(): pl.pallas_call(functools.partial(rs_kernel, plan), out_shape=(pltpu.VMEM(...  235 us
    pallas_call x1, Pallas kernels, all_gather(): pl.pallas_call(functools.partial(ag_kernel, plan), out_shape=[pltpu.VMEM(...  118 us
    pallas_call x1, Pallas kernels, update(): pl.pallas_call(functools.partial(update_kernel, plan), grid=(pl.cdiv(plan...  28 us
    pallas_call x1, Pallas kernels, restore(): pl.pallas_call(functools.partial(restore_kernel, plan), out_shape=[jax.Sh...  12.1 us

profile of v6, /device:TPU:0, one launch (start us, length us, event | category | flops | bytes accessed | tf_op | source)
XLA Modules:
  0.0 399.6 jit_solution(4063556275262913350)
XLA Ops:
  4.1 0.1 stack.35
  4.1 0.1 broadcast_in_dim.10
  4.2 0.1 broadcast_in_dim.11
  4.3 0.1 broadcast_in_dim.12.table
  4.4 0.0 copy-start.3
  4.4 0.8 copy-done.3
  5.2 0.0 copy-start.4
  5.2 0.7 copy-done.4
  5.9 0.0 copy-start.5
  5.9 0.7 copy-done.5
  6.6 0.0 copy-start
  6.6 0.0 copy-start.1
  6.6 0.0 copy-start.2
  6.6 234.6 %reduce_scatter.1 = (f32[8640,128]{1,0:T(8,128)S(1)}, f32[48,720,128]{2,1,0:T(8,128)}) custom-call(f32[24576,128]{1,0:T(8,128)} %bitcast.96, f32[27648,128]{1,0:T(8,128)} %bitcast.95, f32[9216,128]{1,0:T(8,128)} %bitcast.97, f32[36864,128]{1,0:T(8,128)} %bitcast.93, f32[36864,128]{1,0:T(8,128)} %bitcast.94, f32[2,2304]{1,0:T(2,128)S(1)} %bitcast.92, ...), custom_call_target="tpu_custom_call" | custom-call | tf_op jit(solution)/shard_map/reduce_scatter/pallas_call | solution.py:423
  241.2 0.0 copy-done
  241.3 0.0 copy-done.1
  241.3 0.0 copy-done.2
  241.3 28.0 %update.1 = (f32[1082592]{0:T(1024)}, f32[1082592]{0:T(1024)}, f32[1082592]{0:T(1024)}, f32[8896,128]{1,0:T(8,128)S(1)}) custom-call(f32[64,128]{1,0:T(8,128)S(1)} %broadcast_in_dim.12.table, f32[8640,128]{1,0:T(8,128)S(1)} %get-tuple-element.27.g, f32[1082592]{0:T(1024)S(1)} %copy-done, f32[1082592]{0:T(1024)S(1)} %copy-done.1, f32[1082592]{0:T(1024)S(1)} %copy-done.2), custom_call_target="tpu_custom_call" | custom-call | tf_op jit(solution)/shard_map/update/pallas_call | solution.py:667
  269.3 117.5 %all_gather.1 = (bf16[46080,128]{1,0:T(8,128)(2,1)S(1)}, bf16[46080,128]{1,0:T(8,128)(2,1)S(1)}, bf16[46080,128]{1,0:T(8,128)(2,1)S(1)}) custom-call(f32[8896,128]{1,0:T(8,128)S(1)} %get-tuple-element.31.values), custom_call_target="tpu_custom_call" | custom-call | tf_op jit(solution)/shard_map/all_gather/pallas_call | solution.py:568
  386.8 12.1 %restore.1 = (bf16[24576,128]{1,0:T(8,128)(2,1)}, bf16[27648,128]{1,0:T(8,128)(2,1)}, bf16[9216,128]{1,0:T(8,128)(2,1)}, bf16[36864,128]{1,0:T(8,128)(2,1)}, bf1...) custom-call(bf16[46080,128]{1,0:T(8,128)(2,1)S(1)} %get-tuple-element., ...), custom_call_target="tpu_custom_call" | custom-call | tf_op jit(solution)/shard_map/restore/pallas_call | solution.py:614
  399.0 0.6 copy.37
  (3 shorter events, 0.0 us)
Async XLA Ops:
  4.4 0.8 copy-start.3
  5.2 0.7 copy-start.4
  5.9 0.7 copy-start.5
  6.6 234.6 %copy-start = (f32[1082592]{0:T(1024)S(1)}, f32[1082592]{0:T(1024)}, u32[]{:S(2)}) copy-start(f32[1082592]{0:T(1024)} %m.1) | copy-start | bytes 12991108
  6.6 234.6 %copy-start.1 = (f32[1082592]{0:T(1024)S(1)}, f32[1082592]{0:T(1024)}, u32[]{:S(2)}) copy-start(f32[1082592]{0:T(1024)} %v.1) | copy-start | bytes 12991108
  6.6 234.6 %copy-start.2 = (f32[1082592]{0:T(1024)S(1)}, f32[1082592]{0:T(1024)}, u32[]{:S(2)}) copy-start(f32[1082592]{0:T(1024)} %w.1) | copy-start | bytes 12991108

commit v7 on v5

--- a/solution.py
+++ b/solution.py
@@ -40,11 +40,15 @@
             self.starts.append(self.group(r * self.shard // LANES)[0])
             low, size = self.group(((r + 1) * self.shard - 1) // LANES)
             need = max(need, low + size - self.starts[r])
-        self.part = -(-need // (3 * SPLIT * TILE)) * TILE
-        self.unit = SPLIT * self.part
-        self.window = 3 * self.unit
+        step = 3 * HALVES * 3 * TILE
+        self.window = -(-need // step) * step
+        self.unit = self.window // 3
         self.piece = self.unit // HALVES
-        self.small_rows = self.starts[p - 1] + self.window - self.small_row
+        own = [b - a for a, b in zip(self.starts, self.starts[1:] + [self.total // LANES])]
+        self.part = -(-max(own) // (3 * SPLIT * 8)) * 8
+        self.sums = 3 * SPLIT * self.part
+        self.edge = max(8 * nj for _, nj, _ in self.big)
+        self.small_rows = self.starts[p - 1] + self.sums - self.small_row
 
     def group(self, row):
         for n, nj, flat in self.big:
@@ -60,7 +64,7 @@
     def crossing(self):
         out = {}
         for start in self.starts:
-            for lo in range(start, start + self.window, self.part):
+            for lo in range(start, start + self.sums, self.part):
                 cuts = []
                 for t, (x, y) in enumerate(self.spans()):
                     x, y = max(x, lo), min(y, lo + self.part)
@@ -161,14 +165,14 @@
     return (k, (k + 1) % 3, (k + 2) % 3)
 
 
-def arrive(place):
+def arrive(place, others=()):
     barrier = pltpu.get_barrier_semaphore()
-    for peer in [place.partner()] + [place.flipped(d) for d in range(3)]:
+    for peer in [place.partner()] + [place.flipped(d) for d in range(3)] + list(others):
         pl.semaphore_signal(barrier, inc=1, device_id=peer, device_id_type=MESH)
 
 
-def meet():
-    pl.semaphore_wait(pltpu.get_barrier_semaphore(), 4)
+def meet(peers):
+    pl.semaphore_wait(pltpu.get_barrier_semaphore(), peers)
 
 
 def remote(src, dst, send, recv, dev):
@@ -181,8 +185,10 @@
     n_big = len(plan.big)
     n_in = n_big + len(plan.pairs())
     flat, late_ref = refs[n_in:n_in + 2]
-    early, r1, r2, r3, own, oth, small, odd = refs[n_in + 2:n_in + 10]
-    own_sem, oth_sem, d_send, d_recv, s1_send, s1_recv, s2_send, s2_recv, s3_send, s3_recv, tiny_sem = refs[n_in + 10:]
+    early, r1, r2, r3, own, oth, small, odd, edge = refs[n_in + 2:n_in + 11]
+    own_sem, oth_sem, d_send, d_recv, s1_send, s1_recv, s2_send, s2_recv, s3_send, s3_recv, tiny_sem, edge_sem = refs[
+        n_in + 11:
+    ]
     xs = refs[:n_big] + (small,)
     part = plan.part
     wave = 3 * SPLIT
@@ -198,7 +204,7 @@
 
             @pl.when((row >= lo) & (row <= hi - part))
             def _(t=t, lo=lo):
-                issue(xs[t].at[pl.ds(pl.multiple_of(row - lo, TILE), part)], 0, part)
+                issue(xs[t].at[pl.ds(pl.multiple_of(row - lo, 8), part)], 0, part)
 
         for first, cuts in crossing.items():
 
@@ -259,15 +265,19 @@
     def add(dst, *srcs):
         step = 48
 
-        def body(i, _):
-            rows = pl.ds(pl.multiple_of(i * step, TILE), step)
+        def some(rows):
             total = dst[rows, :]
             for s in srcs:
                 total = total + s[rows, :]
             dst[rows, :] = total
+
+        def body(i, _):
+            some(pl.ds(pl.multiple_of(i * step, 8), step))
             return 0
 
         lax.fori_loop(0, part // step, body, 0)
+        if part % step:
+            some(pl.ds(part - part % step, part % step))
 
     def loop(count, f):
         def body(i, _):
@@ -276,7 +286,9 @@
 
         lax.fori_loop(0, count, body, 0)
 
-    arrive(place)
+    me = place.owner(dims_of(0), (0, 0, 0), place.core)
+    after = lax.rem(me + 1, plan.p)
+    arrive(place, [(lax.div(after, 4), lax.rem(after, 4))])
     copies = []
     for m, (x, (_, kept, nj)) in enumerate(zip(refs[n_big:n_in], plan.pairs())):
         dst = odd if m == 0 else small.at[pl.ds(kept, 2 * nj)]
@@ -290,7 +302,7 @@
     for j in range(nj):
         small[kept + 2 * j:kept + 2 * j + 2, :] = odd[:, j * LANES:(j + 1) * LANES]
     loop(DEEP, load)
-    meet()
+    meet(5)
     loop(LEAD, swap)
 
     def first(i):
@@ -353,9 +365,13 @@
 
     loop(2 * wave, third)
 
-    me = place.owner(dims_of(0), (0, 0, 0), place.core)
     first_row = plan.start(me)
-    stored = r1.at[pl.ds(3 * wave, wave)].reshape(plan.window, LANES)
+    stored = r1.at[pl.ds(3 * wave, wave + 1)].reshape((wave + 1) * part, LANES)
+    before = lax.rem(me + plan.p - 1, plan.p)
+    passed = remote(
+        r1.at[3 * wave, pl.ds(0, plan.edge)], edge, edge_sem.at[0], edge_sem.at[1],
+        (lax.div(before, 4), lax.rem(before, 4)),
+    )
 
     def move(nj, base):
         for j in range(nj):
@@ -369,7 +385,15 @@
             add(r1.at[3 * wave + slot], r3.at[slot])
 
         loop(3, fourth)
-        plan.sort(first_row, 3 * s * part, 3 * (s + 1) * part, False, move)
+        if s == 0:
+            passed.start()
+        if s == SPLIT - 1:
+            passed.wait_recv()
+            gap = jnp.where(me == plan.p - 1, plan.sums, plan.start(after) - first_row)
+            for i in range(0, plan.edge, TILE):
+                stored[pl.ds(pl.multiple_of(gap + i, TILE if plan.sums % TILE == 0 else 8), TILE), :] = edge[i:i + TILE, :]
+        end = 3 * (s + 1) * part if s < SPLIT - 1 else plan.window
+        plan.sort(first_row, 3 * s * part, end, False, move)
 
     @pl.when(me == plan.p - 1)
     def _():
@@ -378,6 +402,8 @@
             for layer in range(2):
                 flat[pl.ds(base + row + layer * nj, nj), :] = stored[pl.ds(base + kept + layer, nj, stride=2), :]
 
+    passed.wait_send()
+
     def sent(i):
         k, slot = lax.rem(i, 3), i
         swapped(slot).wait_send()
@@ -398,7 +424,7 @@
 def reduce_scatter(plan, xs):
     dma = pltpu.SemaphoreType.DMA
     wave = 3 * SPLIT
-    slots = [4 * wave, 4 * wave, 2 * wave, wave, DEEP, DEEP]
+    slots = [4 * wave, 4 * wave + 1, 2 * wave, wave, DEEP, DEEP]
     used = (sum(slots) * plan.part * LANES * 4 >> 20) + 2
     g, _ = pl.pallas_call(
         functools.partial(rs_kernel, plan),
@@ -410,9 +436,10 @@
         out_specs=(pl.BlockSpec(memory_space=pltpu.VMEM), ANY),
         scratch_shapes=[pltpu.VMEM((n, plan.part, LANES), F32) for n in slots]
         + [pltpu.VMEM((plan.small_rows, LANES), F32), pltpu.VMEM(xs[len(plan.big)].shape, F32)]
+        + [pltpu.VMEM((plan.edge, LANES), F32)]
         + [dma((DEEP,)), dma((DEEP,))]
         + [dma((n * wave,)) for n in (8, 8, 4, 4, 2, 2, 1, 1)]
-        + [dma((len(plan.pairs()),))],
+        + [dma((len(plan.pairs()),)), dma((2,))],
         compiler_params=pltpu.CompilerParams(
             collective_id=0, has_side_effects=True, vmem_limit_bytes=used << 20
         ),
@@ -487,7 +514,7 @@
     for s in range(HALVES):
         plan.sort(first_row, 3 * s * part, 3 * (s + 1) * part, True, move)
         if s == 0:
-            meet()
+            meet(4)
         for n in range(3):
             for k in range(3):
                 send(k, here, s, n)

time: 378 us -> 377 us (level)
  no operation moved by 1% of the time
where the time goes in v7:
time: 377 us
  Pallas kernels  362 us (96%)
  other arithmetic  7.58 us (2%)
  between operations  4.23 us (1%)
    pallas_call x1, Pallas kernels, reduce_scatter(): pl.pallas_call(functools.partial(rs_kernel, plan), out_shape=(pltpu.VMEM(...  231 us
    pallas_call x1, Pallas kernels, all_gather(): pl.pallas_call(functools.partial(ag_kernel, plan), out_shape=[pltpu.VMEM(...  119 us
    pallas_call x1, Pallas kernels, restore(): pl.pallas_call(functools.partial(restore_kernel, plan), out_shape=[jax.Sh...  12.1 us
    sub x1, other arithmetic, adam_update(): w_new = w - lr * m_hat / (jnp.sqrt(v_hat) + eps)  7.58 us

profile of v7, /device:TPU:0, one launch (start us, length us, event | category | flops | bytes accessed | tf_op | source)
XLA Modules:
  0.0 376.6 jit_solution(1289693562401589207)
XLA Ops:
  4.1 0.0 copy-start.1
  4.2 0.0 copy-start.2
  4.2 231.2 %reduce_scatter.1 = (f32[8640,128]{1,0:T(8,128)S(1)}, f32[48,712,128]{2,1,0:T(8,128)}) custom-call(f32[24576,128]{1,0:T(8,128)} %bitcast.85, f32[27648,128]{1,0:T(8,128)} %bitcast.84, f32[9216,128]{1,0:T(8,128)} %bitcast.86, f32[36864,128]{1,0:T(8,128)} %bitcast.82, f32[36864,128]{1,0:T(8,128)} %bitcast.83, f32[2,2304]{1,0:T(2,128)} %bitcast.90, ...), custom_call_target="tpu_custom_call" | custom-call | tf_op jit(solution)/shard_map/reduce_scatter/pallas_call | solution.py:429
  235.3 0.0 copy-done.1
  235.4 0.0 copy-done.2
  235.4 7.6 %divide_subtract_fusion = (f32[1082592]{0:T(1024)S(1)}, f32[1082592]{0:T(1024)}, f32[1082592]{0:T(1024)}) fusion(f32[1082592]{0:T(1024)S(1)} %copy-done.1, f32[]{:T(128)S(6)} %copy.41, f32[]{:T(128)S(6)} %div.18, f32[]{:T(128)S(6)} %div.17, f32[]{:T(128)S(6)} %copy.38, f32[1105920]{0:T(1024)S(1)} %bitcast.81, s32[]{:T(128)S(6)} %select_n.67, f32[]{:T(128)S(6)} %sub.23, ...), kind=kLoop, calls=%fused_computation.2 | loop fusion | flops 15156288 | bytes 30312612 | tf_op jit(solution)/shard_map/sub | solution.py:634
  242.9 0.0 copy-start
  243.0 1.5 fusion.values
  244.4 0.6 copy-done
  245.0 118.8 %all_gather.1 = (bf16[46080,128]{1,0:T(8,128)(2,1)S(1)}, bf16[46080,128]{1,0:T(8,128)(2,1)S(1)}, bf16[46080,128]{1,0:T(8,128)(2,1)S(1)}) custom-call(f32[8640,128]{1,0:T(8,128)S(1)} %fusion.values), custom_call_target="tpu_custom_call" | custom-call | tf_op jit(solution)/shard_map/all_gather/pallas_call | solution.py:565
  363.9 12.1 %restore.1 = (bf16[24576,128]{1,0:T(8,128)(2,1)}, bf16[27648,128]{1,0:T(8,128)(2,1)}, bf16[9216,128]{1,0:T(8,128)(2,1)}, bf16[36864,128]{1,0:T(8,128)(2,1)}, bf1...) custom-call(bf16[46080,128]{1,0:T(8,128)(2,1)S(1)} %get-tuple-element., ...), custom_call_target="tpu_custom_call" | custom-call | tf_op jit(solution)/shard_map/restore/pallas_call | solution.py:611
  376.0 0.6 copy.37
  (3 shorter events, 0.0 us)
Async XLA Ops:
  4.1 231.2 %copy-start.1 = (f32[1082592]{0:T(1024)S(1)}, f32[1082592]{0:T(1024)}, u32[]{:S(2)}) copy-start(f32[1082592]{0:T(1024)} %param.26) | copy-start | bytes 12991108
  4.2 231.2 %copy-start.2 = (f32[1082592]{0:T(1024)S(1)}, f32[1082592]{0:T(1024)}, u32[]{:S(2)}) copy-start(f32[1082592]{0:T(1024)} %param.25) | copy-start | bytes 12991108
  242.9 2.1 copy-start

commit v8 on v7

--- a/solution.py
+++ b/solution.py
@@ -42,11 +42,11 @@
             need = max(need, low + size - self.starts[r])
         step = 3 * HALVES * 3 * TILE
         self.window = -(-need // step) * step
-        self.unit = self.window // 3
-        self.piece = self.unit // HALVES
         own = [b - a for a, b in zip(self.starts, self.starts[1:] + [self.total // LANES])]
         self.part = -(-max(own) // (3 * SPLIT * 8)) * 8
         self.sums = 3 * SPLIT * self.part
+        self.piece = -(-max(own) // (3 * HALVES * TILE)) * TILE
+        self.unit = HALVES * self.piece
         self.edge = max(8 * nj for _, nj, _ in self.big)
         self.small_rows = self.starts[p - 1] + self.sums - self.small_row
 
@@ -449,13 +449,14 @@
 
 
 def ag_kernel(plan, values, *refs):
-    w_refs, (win, tiny, s_send, s_recv, d_send, d_recv) = refs[:3], refs[3:]
+    w_refs, (win, tiny, edge, s_send, s_recv, d_send, d_recv, edge_sem) = refs[:3], refs[3:]
     part, unit = plan.piece, plan.unit
     place = Place()
     partner = place.partner()
     here = (0, 0, 0)
     me = place.owner(dims_of(0), here, place.core)
-    arrive(place)
+    after, before = lax.rem(me + 1, plan.p), lax.rem(me + plan.p - 1, plan.p)
+    arrive(place, [(lax.div(before, 4), lax.rem(before, 4))])
 
     first_row = plan.start(me)
 
@@ -511,17 +512,39 @@
         i, dst = index(k, e, s), rows_of(k, e, s, 1 - place.core)
         return remote(dst, dst, d_send.at[i], d_recv.at[i], partner)
 
-    for s in range(HALVES):
-        plan.sort(first_row, 3 * s * part, 3 * (s + 1) * part, True, move)
+    gap = jnp.where(me == plan.p - 1, 3 * plan.unit, plan.start(after) - first_row)
+    passed = remote(
+        win.at[pl.ds(pl.multiple_of(gap, TILE), plan.edge)], edge, edge_sem.at[0], edge_sem.at[1],
+        (lax.div(after, 4), lax.rem(after, 4)),
+    )
+    for s in reversed(range(HALVES)):
+        end = 3 * (s + 1) * part if s < HALVES - 1 else plan.window
+        plan.sort(first_row, 3 * s * part, end, False, move)
+        if s == HALVES - 1:
+            meet(5)
+            passed.start()
         if s == 0:
-            meet(4)
+            passed.wait_recv()
+            for r in range(1, plan.p):
+
+                @pl.when(me == r)
+                def _(r=r):
+                    size = plan.group(plan.starts[r])[1]
+                    nj, shape = size // 8, (size, LANES)
+                    row, lane = (lax.broadcasted_iota(jnp.int32, shape, d) for d in range(2))
+                    at = (lax.rem(row, 8) * nj + lax.div(row, 8)) * LANES + lane
+                    cut = r * plan.shard - plan.starts[r] * LANES
+                    rows = pl.ds(0, size)
+                    merged = jnp.where(at < cut, edge[rows, :].astype(F32), win[rows, :].astype(F32))
+                    win[rows, :] = merged.astype(BF)
+
         for n in range(3):
             for k in range(3):
                 send(k, here, s, n)
     for s in range(HALVES):
         for k in range(3):
             share(k, here, s)
-    rows = 3 * TILE
+    rows = TILE
     for s in range(HALVES):
         for k in range(3):
 
@@ -533,7 +556,7 @@
 
             lax.fori_loop(0, part // rows, keep, 0)
     for e in list(slot)[1:]:
-        for s in range(HALVES):
+        for s in reversed(range(HALVES)):
             for k in range(3):
                 arrival(k, e, s).wait_recv()
                 for n in range(1, 3):
@@ -547,16 +570,7 @@
     for copy in sent:
         copy.wait_send()
 
-    for r in range(1, plan.p):
-        size = plan.group(plan.starts[r])[1]
-        nj, shape = size // 8, (size, LANES)
-        row, lane = lax.broadcasted_iota(jnp.int32, shape, 0), lax.broadcasted_iota(jnp.int32, shape, 1)
-        at = (lax.rem(row, 8) * nj + lax.div(row, 8)) * LANES + lane
-        cut = r * plan.shard - plan.starts[r] * LANES
-        gap = plan.starts[r] - plan.starts[r - 1] - plan.window
-        before = w_refs[2][pl.ds(r * unit + gap, size), :]
-        rows = pl.ds(r * unit, size)
-        w_refs[0][rows, :] = jnp.where(at < cut, before.astype(F32), w_refs[0][rows, :].astype(F32)).astype(BF)
+    passed.wait_send()
 
 
 def all_gather(plan, win):
@@ -567,8 +581,10 @@
         out_shape=[pltpu.VMEM((plan.p * plan.unit, LANES), BF)] * 3,
         in_specs=[pl.BlockSpec(memory_space=pltpu.VMEM)],
         out_specs=[pl.BlockSpec(memory_space=pltpu.VMEM)] * 3,
-        scratch_shapes=[pltpu.VMEM((plan.window, LANES), BF), pltpu.VMEM((small_rows(plan), LANES), F32)]
-        + [dma((n,))] * 4,
+        scratch_shapes=[pltpu.VMEM((3 * plan.unit + plan.edge, LANES), BF), pltpu.VMEM((small_rows(plan), LANES), F32)]
+        + [pltpu.VMEM((plan.edge, LANES), BF)]
+        + [dma((n,))] * 4
+        + [dma((2,))],
         compiler_params=pltpu.CompilerParams(collective_id=1, has_side_effects=True, vmem_limit_bytes=8 << 20),
         name="all_gather",
     )(win)

time: 377 us -> 377 us (level)
  no operation moved by 1% of the time
where the time goes in v8:
time: 377 us
  Pallas kernels  361 us (96%)
  other arithmetic  7.58 us (2%)
  between operations  4.23 us (1%)
  local copies, waits for them, and re-layouts  4.18 us (1%)
    pallas_call x1, Pallas kernels, reduce_scatter(): pl.pallas_call(functools.partial(rs_kernel, plan), out_shape=(pltpu.VMEM(...  231 us
    pallas_call x1, Pallas kernels, all_gather(): pl.pallas_call(functools.partial(ag_kernel, plan), out_shape=[pltpu.VMEM(...  118 us
    pallas_call x1, Pallas kernels, restore(): pl.pallas_call(functools.partial(restore_kernel, plan), out_shape=[jax.Sh...  12.1 us
    sub x1, other arithmetic, adam_update(): w_new = w - lr * m_hat / (jnp.sqrt(v_hat) + eps)  7.58 us

profile of v8, /device:TPU:0, one launch (start us, length us, event | category | flops | bytes accessed | tf_op | source)
XLA Modules:
  0.0 377.3 jit_solution(6245566720193587620)
XLA Ops:
  4.1 0.0 copy-start.1
  4.2 0.0 copy-start.2
  4.2 231.2 %reduce_scatter.1 = (f32[8640,128]{1,0:T(8,128)S(1)}, f32[48,712,128]{2,1,0:T(8,128)}) custom-call(f32[24576,128]{1,0:T(8,128)} %bitcast.85, f32[27648,128]{1,0:T(8,128)} %bitcast.84, f32[9216,128]{1,0:T(8,128)} %bitcast.86, f32[36864,128]{1,0:T(8,128)} %bitcast.82, f32[36864,128]{1,0:T(8,128)} %bitcast.83, f32[2,2304]{1,0:T(2,128)} %bitcast.90, ...), custom_call_target="tpu_custom_call" | custom-call | tf_op jit(solution)/shard_map/reduce_scatter/pallas_call | solution.py:429
  235.3 0.0 copy-done.1
  235.4 0.0 copy-done.2
  235.4 7.6 %divide_subtract_fusion = (f32[1082592]{0:T(1024)S(1)}, f32[1082592]{0:T(1024)}, f32[1082592]{0:T(1024)}) fusion(f32[1082592]{0:T(1024)S(1)} %copy-done.1, f32[]{:T(128)S(6)} %copy.41, f32[]{:T(128)S(6)} %div.18, f32[]{:T(128)S(6)} %div.17, f32[]{:T(128)S(6)} %copy.38, f32[1105920]{0:T(1024)S(1)} %bitcast.81, s32[]{:T(128)S(6)} %select_n.67, f32[]{:T(128)S(6)} %sub.23, ...), kind=kLoop, calls=%fused_computation.2 | loop fusion | flops 15156288 | bytes 30312612 | tf_op jit(solution)/shard_map/sub | solution.py:650
  242.9 0.0 copy-start
  243.0 2.1 copy-done
  245.0 1.5 fusion.values
  246.5 118.0 %all_gather.1 = (bf16[45568,128]{1,0:T(8,128)(2,1)S(1)}, bf16[45568,128]{1,0:T(8,128)(2,1)S(1)}, bf16[45568,128]{1,0:T(8,128)(2,1)S(1)}) custom-call(f32[8640,128]{1,0:T(8,128)S(1)} %fusion.values), custom_call_target="tpu_custom_call" | custom-call | tf_op jit(solution)/shard_map/all_gather/pallas_call | solution.py:579
  364.5 12.1 %restore.1 = (bf16[24576,128]{1,0:T(8,128)(2,1)}, bf16[27648,128]{1,0:T(8,128)(2,1)}, bf16[9216,128]{1,0:T(8,128)(2,1)}, bf16[36864,128]{1,0:T(8,128)(2,1)}, bf1...) custom-call(bf16[45568,128]{1,0:T(8,128)(2,1)S(1)} %get-tuple-element., ...), custom_call_target="tpu_custom_call" | custom-call | tf_op jit(solution)/shard_map/restore/pallas_call | solution.py:627
  376.7 0.6 copy.37
  (3 shorter events, 0.0 us)
Async XLA Ops:
  4.1 231.2 %copy-start.1 = (f32[1082592]{0:T(1024)S(1)}, f32[1082592]{0:T(1024)}, u32[]{:S(2)}) copy-start(f32[1082592]{0:T(1024)} %param.26) | copy-start | bytes 12991108
  4.2 231.2 %copy-start.2 = (f32[1082592]{0:T(1024)S(1)}, f32[1082592]{0:T(1024)}, u32[]{:S(2)}) copy-start(f32[1082592]{0:T(1024)} %param.25) | copy-start | bytes 12991108
  242.9 2.1 copy-start

commit v9 on v8

--- a/solution.py
+++ b/solution.py
@@ -585,7 +585,7 @@
         + [pltpu.VMEM((plan.edge, LANES), BF)]
         + [dma((n,))] * 4
         + [dma((2,))],
-        compiler_params=pltpu.CompilerParams(collective_id=1, has_side_effects=True, vmem_limit_bytes=8 << 20),
+        compiler_params=pltpu.CompilerParams(collective_id=1, has_side_effects=True, vmem_limit_bytes=6 << 20),
         name="all_gather",
     )(win)
 

time: 377 us -> 376 us (level)
  no operation moved by 1% of the time
where the time goes in v9:
time: 376 us
  Pallas kernels  361 us (96%)
  other arithmetic  7.58 us (2%)
  between operations  4.23 us (1%)
    pallas_call x1, Pallas kernels, reduce_scatter(): pl.pallas_call(functools.partial(rs_kernel, plan), out_shape=(pltpu.VMEM(...  231 us
    pallas_call x1, Pallas kernels, all_gather(): pl.pallas_call(functools.partial(ag_kernel, plan), out_shape=[pltpu.VMEM(...  118 us
    pallas_call x1, Pallas kernels, restore(): pl.pallas_call(functools.partial(restore_kernel, plan), out_shape=[jax.Sh...  12.1 us
    sub x1, other arithmetic, adam_update(): w_new = w - lr * m_hat / (jnp.sqrt(v_hat) + eps)  7.58 us

profile of v9, /device:TPU:0, one launch (start us, length us, event | category | flops | bytes accessed | tf_op | source)
XLA Modules:
  0.0 375.8 jit_solution(5431293194979689191)
XLA Ops:
  4.1 0.0 copy-start.1
  4.2 0.0 copy-start.2
  4.2 231.2 %reduce_scatter.1 = (f32[8640,128]{1,0:T(8,128)S(1)}, f32[48,712,128]{2,1,0:T(8,128)}) custom-call(f32[24576,128]{1,0:T(8,128)} %bitcast.85, f32[27648,128]{1,0:T(8,128)} %bitcast.84, f32[9216,128]{1,0:T(8,128)} %bitcast.86, f32[36864,128]{1,0:T(8,128)} %bitcast.82, f32[36864,128]{1,0:T(8,128)} %bitcast.83, f32[2,2304]{1,0:T(2,128)} %bitcast.90, ...), custom_call_target="tpu_custom_call" | custom-call | tf_op jit(solution)/shard_map/reduce_scatter/pallas_call | solution.py:429
  235.3 0.0 copy-done.1
  235.4 0.0 copy-done.2
  235.4 7.6 %divide_subtract_fusion = (f32[1082592]{0:T(1024)S(1)}, f32[1082592]{0:T(1024)}, f32[1082592]{0:T(1024)}) fusion(f32[1082592]{0:T(1024)S(1)} %copy-done.1, f32[]{:T(128)S(6)} %copy.41, f32[]{:T(128)S(6)} %div.18, f32[]{:T(128)S(6)} %div.17, f32[]{:T(128)S(6)} %copy.38, f32[1105920]{0:T(1024)S(1)} %bitcast.81, s32[]{:T(128)S(6)} %select_n.67, f32[]{:T(128)S(6)} %sub.23, ...), kind=kLoop, calls=%fused_computation.2 | loop fusion | flops 15156288 | bytes 30312612 | tf_op jit(solution)/shard_map/sub | solution.py:650
  242.9 0.0 copy-start
  243.0 1.5 fusion.values
  244.4 0.6 copy-done
  245.0 118.0 %all_gather.1 = (bf16[45568,128]{1,0:T(8,128)(2,1)S(1)}, bf16[45568,128]{1,0:T(8,128)(2,1)S(1)}, bf16[45568,128]{1,0:T(8,128)(2,1)S(1)}) custom-call(f32[8640,128]{1,0:T(8,128)S(1)} %fusion.values), custom_call_target="tpu_custom_call" | custom-call | tf_op jit(solution)/shard_map/all_gather/pallas_call | solution.py:579
  363.0 12.1 %restore.1 = (bf16[24576,128]{1,0:T(8,128)(2,1)}, bf16[27648,128]{1,0:T(8,128)(2,1)}, bf16[9216,128]{1,0:T(8,128)(2,1)}, bf16[36864,128]{1,0:T(8,128)(2,1)}, bf1...) custom-call(bf16[45568,128]{1,0:T(8,128)(2,1)S(1)} %get-tuple-element., ...), custom_call_target="tpu_custom_call" | custom-call | tf_op jit(solution)/shard_map/restore/pallas_call | solution.py:627
  375.2 0.6 copy.37
  (3 shorter events, 0.0 us)
Async XLA Ops:
  4.1 231.2 %copy-start.1 = (f32[1082592]{0:T(1024)S(1)}, f32[1082592]{0:T(1024)}, u32[]{:S(2)}) copy-start(f32[1082592]{0:T(1024)} %param.26) | copy-start | bytes 12991108
  4.2 231.2 %copy-start.2 = (f32[1082592]{0:T(1024)S(1)}, f32[1082592]{0:T(1024)}, u32[]{:S(2)}) copy-start(f32[1082592]{0:T(1024)} %param.25) | copy-start | bytes 12991108
  242.9 2.1 copy-start
